TPU v7x, 128 devices: a whole 4x4x4 slice. The times are simulated.
128 devices in a mesh: leaf: 128 (over x, z, y, core).
Axes of the slice: x: 4, y: 4, z: 4, core: 2. Of those that a mesh axis runs over, the one named last changes fastest.
Arguments:
- slip: bfloat16 [128, 32768], P(None, 'leaf'), may hold values from -6 to 6
- to_multipole: bfloat16 [121, 128], replicated, may hold values from -0.5 to 0.5
- up_shift: float32 [2, 121, 121], replicated, may hold values from -0.375 to 0.375
- down_shift: float32 [2, 121, 121], replicated, may hold values from -0.5 to 0.5
- sibling_far: float32 [2, 121, 121], replicated, may hold values from -0.5 to 0.5
- leaf_far: bfloat16 [27, 121, 121], replicated, may hold values from -0.25 to 0.25
- to_stress: bfloat16 [128, 121], replicated, may hold values from -0.125 to 0.125
- near_blocks: bfloat16 [9, 128, 128], replicated, may hold values from -0.1875 to 0.1875
- send_cells: int32 [128, 16384], P('leaf'), may hold values from 0 to 255, as said below
- far_list: int32 [27, 32768], P(None, 'leaf'), may hold values from 0 to 16639, as said below
- near_list: int32 [9, 32768], P(None, 'leaf'), may hold values from 0 to 319, as said below
Outputs:
- stress: float32 [128, 32768], P(None, 'leaf')
Inputs may be any that keep to these rules, and one draw needn't show every extreme that they name: `send_cells`: row q holds, in positions d * 128 to (d + 1) * 128 - 1, 128 distinct cells of device q (numbered within that device) listed for receiving device d. `far_list`: an entry v below 256 names a cell of the target's own device. Otherwise v - 256 = q * 128 + s names slot s of device q's list for the target's device, q is not the target's device, s < 128 when q lies within 4 devices of it and s < 32 when it lies farther; in every draw some entry names slot 127 of a device within 4, and some names slot 31 of a farther device. `near_list`: an entry w names the cell w - 32 counted from the first cell of the target's device, so that positions before 0 and from 256 on lie on the neighbouring devices (zeros outside the fault); entry 4 is the target itself.
All inputs are finite; a program needn't handle non-finite values.
Results may differ from a plain program's by a relative error of at most 0.0031.
Values may be sent and summed in bfloat16 or wider, within the bound.
A program may use at most 64 MiB of HBM per device.

v0:
```python
import jax
import jax.numpy as jnp
from jax import lax
from jax.sharding import PartitionSpec as P

NEAR = 9
TYPES = 27
NEAR_PEERS = 4
HALO = 32
CAP_NEAR = 128
CAP_FAR = 32


def with_halo(block, sides, width):
    for axis, dim in sides:
        count = lax.axis_size(axis)
        forward = [(i, i + 1) for i in range(count - 1)]
        backward = [(target, source) for source, target in forward]
        low = lax.ppermute(
            lax.slice_in_dim(block, block.shape[dim] - width, None, axis=dim), axis, forward
        )
        high = lax.ppermute(lax.slice_in_dim(block, 0, width, axis=dim), axis, backward)
        block = jnp.concatenate([low, block, high], axis=dim)
    return block


def shifted(shard, axis, by):
    length = lax.axis_size(axis)
    pairs = [(i, i + by) for i in range(length) if 0 <= i + by < length]
    return lax.ppermute(shard, axis, pairs)


def swapped(block, axis, stride):
    count = lax.axis_size(axis)
    route = []
    for low in range(count):
        high = low | 1 << stride
        if high != low and high < count:
            route += [(low, high), (high, low)]
    return lax.ppermute(block, axis, route)


def pair_up(up_shift, lower, upper):
    precise = lax.Precision.HIGHEST
    return jnp.dot(up_shift[0], lower, precision=precise) + jnp.dot(
        up_shift[1], upper, precision=precise
    )


def body(
    slip,
    to_multipole,
    up_shift,
    down_shift,
    sibling_far,
    leaf_far,
    to_stress,
    near_blocks,
    send_cells,
    far_list,
    near_list,
):
    precise = lax.Precision.HIGHEST
    cells_here = slip.shape[1]
    coef_count = to_multipole.shape[0]
    devices_all = lax.axis_size("leaf")
    own_index = lax.axis_index("leaf")
    multipole = jnp.dot(to_multipole, slip, preferred_element_type=jnp.float32).astype(jnp.bfloat16)
    extended = with_halo(slip, (("leaf", 1),), HALO)
    near_cols = jnp.take(extended, near_list.reshape(-1), axis=1).reshape(
        extended.shape[0], NEAR, cells_here
    )
    near_part = jnp.einsum(
        "kij,jkc->ic", near_blocks, near_cols, preferred_element_type=jnp.float32
    )
    send_row = send_cells[0]
    offsets = list(range(-NEAR_PEERS, 0)) + list(range(1, NEAR_PEERS + 1))
    pieces = [multipole]
    for offset in offsets:
        chosen = lax.dynamic_slice_in_dim(send_row, (own_index - offset) * CAP_NEAR, CAP_NEAR)
        pieces.append(shifted(jnp.take(multipole, chosen, axis=1), "leaf", -offset))
    far_cells = send_row.reshape(devices_all, CAP_NEAR)[:, :CAP_FAR].reshape(-1)
    pieces.append(
        lax.all_to_all(
            jnp.take(multipole, far_cells, axis=1), "leaf", split_axis=1, concat_axis=1, tiled=True
        )
    )
    sources = jnp.concatenate(pieces, axis=1)
    relative = far_list - cells_here
    sender = relative // CAP_NEAR
    position = relative % CAP_NEAR
    offset_all = sender - own_index
    buffer_pos = jnp.where(offset_all < 0, offset_all + NEAR_PEERS, offset_all + NEAR_PEERS - 1)
    nearby = jnp.abs(offset_all) <= NEAR_PEERS
    close_at = cells_here + buffer_pos * CAP_NEAR + position
    far_at = cells_here + 2 * NEAR_PEERS * CAP_NEAR + sender * CAP_FAR + position
    mapped = jnp.where(far_list < cells_here, far_list, jnp.where(nearby, close_at, far_at))
    leaf_cols = jnp.take(sources, mapped.reshape(-1), axis=1).reshape(coef_count, TYPES, cells_here)
    leaf_sum = jnp.einsum("tij,jtc->ic", leaf_far, leaf_cols, preferred_element_type=jnp.float32)
    local_levels = cells_here.bit_length() - 1
    aggregates = [multipole.astype(jnp.float32)]
    for height in range(local_levels):
        below = aggregates[-1]
        aggregates.append(pair_up(up_shift, below[:, 0::2], below[:, 1::2]))
    root_sum = aggregates[-1]
    tree_bits = devices_all.bit_length() - 1
    siblings = []
    current = root_sum
    for tree_bit in range(tree_bits):
        partner = swapped(current, "leaf", tree_bit)
        siblings.append(partner)
        if tree_bit + 1 < tree_bits:
            branch = own_index >> tree_bit & 1
            lower = jnp.where(branch == 0, current, partner)
            upper = jnp.where(branch == 0, partner, current)
            current = pair_up(up_shift, lower, upper)
    expansion = jnp.zeros((coef_count, 1), jnp.float32)
    for tree_bit in reversed(range(tree_bits)):
        branch = own_index >> tree_bit & 1
        down_pick = lax.dynamic_index_in_dim(down_shift, branch, 0, keepdims=False)
        far_pick = lax.dynamic_index_in_dim(sibling_far, branch, 0, keepdims=False)
        expansion = jnp.dot(down_pick, expansion, precision=precise) + jnp.dot(
            far_pick, siblings[tree_bit], precision=precise
        )
    for height in reversed(range(local_levels)):
        left_part = jnp.dot(down_shift[0], expansion, precision=precise)
        right_part = jnp.dot(down_shift[1], expansion, precision=precise)
        if height >= 1:
            level_sums = aggregates[height]
            left_part = left_part + jnp.dot(sibling_far[0], level_sums[:, 1::2], precision=precise)
            right_part = right_part + jnp.dot(
                sibling_far[1], level_sums[:, 0::2], precision=precise
            )
        expansion = jnp.stack([left_part, right_part], axis=-1).reshape(coef_count, -1)
    local_exp = (expansion + leaf_sum).astype(jnp.bfloat16)
    return jnp.dot(to_stress, local_exp, preferred_element_type=jnp.float32) + near_part


def solution(mesh):
    return jax.shard_map(
        body,
        mesh=mesh,
        in_specs=(
            P(None, "leaf"),
            P(),
            P(),
            P(),
            P(),
            P(),
            P(),
            P(),
            P("leaf", None),
            P(None, "leaf"),
            P(None, "leaf"),
        ),
        out_specs=P(None, "leaf"),
        check_vma=False,
    )
```

profile of v0, /device:TPU:7, one launch (start us, length us, event | category | flops | bytes accessed | tf_op | source)
XLA Modules:
  0.0 167.8 jit_solution(13283745522814006364)
XLA Ops:
  0.0 0.9 compare_and_fusion.3
  0.9 1.0 convolution_convert_fusion
  2.0 0.7 gather_fusion.3
  3.4 4.8 %collective-permute-start.7 = (bf16[121,128]{0,1:T(8,128)(2,1)}, bf16[121,128]{0,1:T(8,128)(2,1)}, u32[]{:S(2)}, u32[]{:S(2)}) collective-permute-start(bf16[121,128]{0,1:T(8,128)(2,1)} %select_bitcast_fusion.7), channel_id=1, source_target_pairs={{0,4},{1,5},{2,6},{3,7},{4,8},{5,9},{6,10},{7,11},{8,12},{9,13},{1... | collective-permute-start | bytes 92936 | tf_op jit(solution)/shard_map/ppermute | solution.py:30
  8.3 0.7 gather_fusion.4
  9.7 4.1 %collective-permute-start.8 = (bf16[121,128]{0,1:T(8,128)(2,1)}, bf16[121,128]{0,1:T(8,128)(2,1)}, u32[]{:S(2)}, u32[]{:S(2)}) collective-permute-start(bf16[121,128]{0,1:T(8,128)(2,1)} %select_bitcast_fusion.6), channel_id=1, source_target_pairs={{0,3},{1,4},{2,5},{3,6},{4,7},{5,8},{6,9},{7,10},{8,11},{9,12},{10... | collective-permute-start | bytes 92936 | tf_op jit(solution)/shard_map/ppermute | solution.py:30
  15.3 3.2 %collective-permute-start.9 = (bf16[121,128]{0,1:T(8,128)(2,1)}, bf16[121,128]{0,1:T(8,128)(2,1)}, u32[]{:S(2)}, u32[]{:S(2)}) collective-permute-start(bf16[121,128]{0,1:T(8,128)(2,1)} %select_bitcast_fusion.5), channel_id=1, source_target_pairs={{0,2},{1,3},{2,4},{3,5},{4,6},{5,7},{6,8},{7,9},{8,10},{9,11},{10,... | collective-permute-start | bytes 92936 | tf_op jit(solution)/shard_map/ppermute | solution.py:30
  18.6 12.1 %gather_fusion = bf16[4096,121]{1,0:T(8,128)(2,1)S(1)} fusion(bf16[121,256]{0,1:T(8,128)(2,1)S(1)} %copy.62, s32[4096]{0:T(1024)S(1)} %broadcast_clamp_fusion), kind=kCustom, calls=%fused_computation.8 | custom fusion | bytes 1998848 | tf_op jit(solution)/shard_map/jit(_take)/gather | solution.py:85
  30.8 2.0 %broadcast_select_fusion = bf16[121,128,32]{0,2,1:T(8,128)(2,1)} fusion(bf16[121,128,32]{0,2,1:T(8,128)(2,1)S(1)} %bitcast.524, pred[128,32]{1,0:T(8,128)(4,1)S(1)} %compare_and_fusion), kind=kLoop, calls=%fused_computation.125 | loop fusion | flops 495616 | bytes 1986560 | tf_op jit(solution)/shard_map/jit(_take)/select_n | solution.py:85
  32.8 9.9 %all-to-all-start = ((bf16[121,128,32]{0,2,1:T(8,128)(2,1)}), bf16[121,128,32]{0,2,1:T(8,128)(2,1)}, u32[]{:S(2)}, u32[]{:S(2)}) async-start(bf16[121,128,32]{0,2,1:T(8,128)(2,1)} %broadcast_select_fusion), calls=%async_computation | async-start | bytes 2097152 | tf_op jit(solution)/shard_map/all_to_all | solution.py:84
  42.7 1.2 slice.52
  43.9 1.2 slice.54
  50.4 3.1 %collective-permute-start.15 = (bf16[128,32]{0,1:T(8,128)(2,1)}, bf16[128,32]{0,1:T(8,128)(2,1)}, u32[]{:S(2)}, u32[]{:S(2)}) collective-permute-start(bf16[128,32]{0,1:T(8,128)(2,1)} %get-tuple-element.58), channel_id=1, source_target_pairs={{0,1},{1,2},{2,3},{3,4},{4,5},{5,6},{6,7},{7,8},{8,9},{9,10},{10,1... | collective-permute-start | bytes 24584 | tf_op jit(solution)/shard_map/ppermute | solution.py:19
  53.6 0.7 gather_fusion.6
  54.3 0.7 gather_fusion.7
  55.0 0.7 gather_fusion.8
  55.7 0.7 gather_fusion.9
  56.4 0.7 gather_fusion.10
  61.3 1.7 %fusion.116 = (f32[1,121,121]{2,0,1:T(1,128)S(1)}, f32[1,121,121]{2,0,1:T(1,128)S(1)}, f32[1,121,121]{2,0,1:T(1,128)S(1)}, f32[1,121,121]{2,0,1:T(1,128)S(1)}, f...) fusion(f32[2,121,121]{2,0,1:T(2,128)S(1)} %copy-done.1, ...), kind=kLoop, calls=%fused_computation.300 | loop fusion | bytes 2108332 | tf_op jit(solution)/shard_map/slice | solution.py:130
  64.1 1.3 collective-permute-start.1
  67.0 2.6 %collective-permute-start.2 = (f32[121,1]{0,1:T(1,128)S(1)}, f32[121,1]{0,1:T(1,128)S(1)}, u32[]{:S(2)}, u32[]{:S(2)}) collective-permute-start(f32[121,1]{0,1:T(1,128)S(1)} %fusion.61), channel_id=1, source_target_pairs={{0,4},{4,0},{1,5},{5,1},{2,6},{6,2},{3,7},{7,3},{8,12},{12,8},{9,1... | collective-permute-start | bytes 1460 | tf_op jit(solution)/shard_map/ppermute | solution.py:40
  69.5 0.8 convolution_bitcast_fusion.34
  71.4 1.5 collective-permute-start.3
  74.0 0.8 fusion.57
  74.8 3.3 %collective-permute-start.4 = (f32[121,1]{0,1:T(1,128)}, f32[121,1]{0,1:T(1,128)}, u32[]{:S(2)}, u32[]{:S(2)}) collective-permute-start(f32[121,1]{0,1:T(1,128)} %fusion.57), channel_id=1, source_target_pairs={{0,16},{16,0},{1,17},{17,1},{2,18},{18,2},{3,19},{19,3},{4,20},{20... | collective-permute-start | bytes 1460 | tf_op jit(solution)/shard_map/ppermute | solution.py:40
  78.1 1.0 collective-permute-done.4
  79.1 0.8 convolution_bitcast_fusion.22
  79.9 0.9 fusion.55
  81.3 1.4 pad_clamp_fusion
  83.6 1.3 collective-permute-start.6
  84.9 0.7 pad_clamp_fusion.1
  85.6 2.1 %collective-permute-done.6 = f32[121,1]{0,1:T(1,128)S(1)} collective-permute-done((f32[121,1]{0,1:T(1,128)S(1)}, f32[121,1]{0,1:T(1,128)S(1)}, u32[]{:S(2)}, u32[]{:S(2)}) %collective-permute-start.6) | collective-permute-done | bytes 516 | tf_op jit(solution)/shard_map/ppermute | solution.py:40
  87.7 8.2 %collective-permute-start.16 = (bf16[128,32]{0,1:T(8,128)(2,1)}, bf16[128,32]{0,1:T(8,128)(2,1)S(1)}, u32[]{:S(2)}, u32[]{:S(2)}) collective-permute-start(bf16[128,32]{0,1:T(8,128)(2,1)} %get-tuple-element.59), channel_id=1, source_target_pairs={{1,0},{2,1},{3,2},{4,3},{5,4},{6,5},{7,6},{8,7},{9,8},{10,9},{11,1... | collective-permute-start | bytes 24584 | tf_op jit(solution)/shard_map/ppermute | solution.py:22
  95.9 1.0 fusion.51
  96.9 1.1 convolution_bitcast_fusion.18
  98.0 1.1 fusion.49
  99.2 0.8 fusion.47
  100.3 0.9 fusion.45
  101.4 0.8 fusion.43
  102.5 0.9 fusion.41
  103.6 0.8 fusion.39
  104.9 0.9 fusion.37
  105.8 0.9 fusion.35
  107.1 0.9 fusion.32
  108.0 0.9 fusion.31
  109.4 0.9 fusion.29
  110.3 0.9 fusion.28
  111.6 0.9 fusion.26
  112.5 0.9 fusion.25
  117.2 3.0 %collective-permute-start.10 = (bf16[121,128]{0,1:T(8,128)(2,1)S(1)}, bf16[121,128]{0,1:T(8,128)(2,1)S(1)}, u32[]{:S(2)}, u32[]{:S(2)}) collective-permute-start(bf16[121,128]{0,1:T(8,128)(2,1)S(1)} %copy-done.15), channel_id=1, source_target_pairs={{0,1},{1,2},{2,3},{3,4},{4,5},{5,6},{6,7},{7,8},{8,9},{9,10},{10,1... | collective-permute-start | bytes 92936 | tf_op jit(solution)/shard_map/ppermute | solution.py:30
  120.2 1.9 %collective-permute-start.11 = (bf16[121,128]{0,1:T(8,128)(2,1)S(1)}, bf16[121,128]{0,1:T(8,128)(2,1)S(1)}, u32[]{:S(2)}, u32[]{:S(2)}) collective-permute-start(bf16[121,128]{0,1:T(8,128)(2,1)S(1)} %copy-done.14), channel_id=1, source_target_pairs={{1,0},{2,1},{3,2},{4,3},{5,4},{6,5},{7,6},{8,7},{9,8},{10,9},{11,1... | collective-permute-start | bytes 92936 | tf_op jit(solution)/shard_map/ppermute | solution.py:30
  122.8 4.7 %gather_fusion.2 = bf16[2304,128]{1,0:T(8,128)(2,1)S(1)} fusion(bf16[128,320]{0,1:T(8,128)(2,1)S(1)} %pad_maximum_fusion.1, s32[3072]{0:T(1024)S(1)} %pad_clamp_fusion.1), kind=kCustom, calls=%fused_computation.10 | custom fusion | bytes 1188864 | tf_op jit(solution)/shard_map/jit(_take)/gather | solution.py:70
  127.5 1.5 convolution_bitcast_fusion
  129.0 7.0 %collective-permute-start.12 = (bf16[121,128]{0,1:T(8,128)(2,1)S(1)}, bf16[121,128]{0,1:T(8,128)(2,1)S(1)}, u32[]{:S(2)}, u32[]{:S(2)}) collective-permute-start(bf16[121,128]{0,1:T(8,128)(2,1)S(1)} %copy-done.13), channel_id=1, source_target_pairs={{2,0},{3,1},{4,2},{5,3},{6,4},{7,5},{8,6},{9,7},{10,8},{11,9},{12,... | collective-permute-start | bytes 92936 | tf_op jit(solution)/shard_map/ppermute | solution.py:30
  136.1 0.8 constant_dynamic-update-slice_fusion.8
  136.8 3.8 %collective-permute-start.13 = (bf16[121,128]{0,1:T(8,128)(2,1)S(1)}, bf16[121,128]{0,1:T(8,128)(2,1)S(1)}, u32[]{:S(2)}, u32[]{:S(2)}) collective-permute-start(bf16[121,128]{0,1:T(8,128)(2,1)S(1)} %copy-done.12), channel_id=1, source_target_pairs={{3,0},{4,1},{5,2},{6,3},{7,4},{8,5},{9,6},{10,7},{11,8},{12,9},{13... | collective-permute-start | bytes 92936 | tf_op jit(solution)/shard_map/ppermute | solution.py:30
  140.7 0.8 constant_dynamic-update-slice_fusion.7
  141.4 4.2 %collective-permute-start.14 = (bf16[121,128]{0,1:T(8,128)(2,1)S(1)}, bf16[121,128]{0,1:T(8,128)(2,1)S(1)}, u32[]{:S(2)}, u32[]{:S(2)}) collective-permute-start(bf16[121,128]{0,1:T(8,128)(2,1)S(1)} %copy-done.11), channel_id=1, source_target_pairs={{4,0},{5,1},{6,2},{7,3},{8,4},{9,5},{10,6},{11,7},{12,8},{13,9},{1... | collective-permute-start | bytes 92936 | tf_op jit(solution)/shard_map/ppermute | solution.py:30
  145.6 0.8 constant_dynamic-update-slice_fusion.6
  146.5 1.7 %collective-permute-done.14 = bf16[121,128]{0,1:T(8,128)(2,1)S(1)} collective-permute-done((bf16[121,128]{0,1:T(8,128)(2,1)S(1)}, bf16[121,128]{0,1:T(8,128)(2,1)S(1)}, u32[]{:S(2)}, u32[]{:S(2)}) %collective-permute-start.14) | collective-permute-done | bytes 31008 | tf_op jit(solution)/shard_map/ppermute | solution.py:30
  148.2 1.4 constant_dynamic-update-slice_fusion
  149.6 14.8 %gather_fusion.1 = bf16[6912,121]{1,0:T(8,128)(2,1)} fusion(bf16[121,5376]{0,1:T(8,128)(2,1)S(1)} %constant_dynamic-update-slice_fusion, s32[7168]{0:T(1024)S(1)} %copy-done.6), kind=kCustom, calls=%fused_computation.9 | custom fusion | bytes 3373056 | tf_op jit(solution)/shard_map/jit(_take)/gather | solution.py:98
  164.3 2.7 %fusion.6 = f32[128,256]{0,1:T(8,128)S(1)} fusion(f32[256,128]{1,0:T(8,128)S(1)} %convolution_bitcast_fusion, bf16[128,121]{1,0:T(8,128)(2,1)S(1)} %copy-done.27, f32[121,256]{0,1:T(8,128)S(1)} %bitcast.535, bf16[27,121,121]{2,1,0:T(8,128)(2,1)S(1)} %copy-done, bf16[121,27,256]{0,2,1:T(8,128)(2,1)} %bitcast.525, pred[27,256]{1,0:T(8,128)(4,1)S(1)} %copy-done.21), kind=kOutput, calls=%fused_computation.17 | convolution fusion | flops 211258112 | bytes 2887254 | tf_op jit(solution)/shard_map/dot_general | solution.py:136
  167.0 0.8 copy.66
  (189 shorter events, 26.1 us)
Async XLA Ops:
  0.0 164.3 %copy-start = (bf16[27,121,121]{2,1,0:T(8,128)(2,1)S(1)}, bf16[27,121,121]{2,1,0:T(8,128)(2,1)}, u32[]{:S(2)}) copy-start(bf16[27,121,121]{2,1,0:T(8,128)(2,1)} %param.18) | copy-start | bytes 2371846
  0.0 18.4 %copy-start.3 = (s32[1,16384]{1,0:T(1,128)S(1)}, s32[1,16384]{1,0:T(1,128)}, u32[]{:S(2)}) copy-start(s32[1,16384]{1,0:T(1,128)} %param.21) | copy-start | bytes 196612
  3.4 125.6 %collective-permute-start.7 = (bf16[121,128]{0,1:T(8,128)(2,1)}, bf16[121,128]{0,1:T(8,128)(2,1)}, u32[]{:S(2)}, u32[]{:S(2)}) collective-permute-start(bf16[121,128]{0,1:T(8,128)(2,1)} %select_bitcast_fusion.7), channel_id=1, source_target_pairs={{0,4},{1,5},{2,6},{3,7},{4,8},{5,9},{6,10},{7,11},{8,12},{9,13},{1... | collective-permute-start | bytes 92936 | tf_op jit(solution)/shard_map/ppermute | solution.py:30
  9.7 127.2 %collective-permute-start.8 = (bf16[121,128]{0,1:T(8,128)(2,1)}, bf16[121,128]{0,1:T(8,128)(2,1)}, u32[]{:S(2)}, u32[]{:S(2)}) collective-permute-start(bf16[121,128]{0,1:T(8,128)(2,1)} %select_bitcast_fusion.6), channel_id=1, source_target_pairs={{0,3},{1,4},{2,5},{3,6},{4,7},{5,8},{6,9},{7,10},{8,11},{9,12},{10... | collective-permute-start | bytes 92936 | tf_op jit(solution)/shard_map/ppermute | solution.py:30
  15.3 126.2 %collective-permute-start.9 = (bf16[121,128]{0,1:T(8,128)(2,1)}, bf16[121,128]{0,1:T(8,128)(2,1)}, u32[]{:S(2)}, u32[]{:S(2)}) collective-permute-start(bf16[121,128]{0,1:T(8,128)(2,1)} %select_bitcast_fusion.5), channel_id=1, source_target_pairs={{0,2},{1,3},{2,4},{3,5},{4,6},{5,7},{6,8},{7,9},{8,10},{9,11},{10,... | collective-permute-start | bytes 92936 | tf_op jit(solution)/shard_map/ppermute | solution.py:30
  32.8 12.3 %copy-start.5 = (f32[2,121,121]{2,0,1:T(2,128)S(1)}, f32[2,121,121]{2,0,1:T(2,128)}, u32[]{:S(2)}) copy-start(f32[2,121,121]{2,0,1:T(2,128)} %param.15) | copy-start | bytes 351388
  32.8 115.4 %all-to-all-start = ((bf16[121,128,32]{0,2,1:T(8,128)(2,1)}), bf16[121,128,32]{0,2,1:T(8,128)(2,1)}, u32[]{:S(2)}, u32[]{:S(2)}) async-start(bf16[121,128,32]{0,2,1:T(8,128)(2,1)} %broadcast_select_fusion), calls=%async_computation | async-start | bytes 2097152 | tf_op jit(solution)/shard_map/all_to_all | solution.py:84
  42.7 7.0 %copy-start.4 = (bf16[128,256]{1,0:T(8,128)(2,1)S(1)}, bf16[128,256]{1,0:T(8,128)(2,1)}, u32[]{:S(2)}) copy-start(bf16[128,256]{1,0:T(8,128)(2,1)} %param.13) | copy-start | bytes 196612
  46.2 10.9 %copy-start.10 = (s32[27,256]{1,0:T(8,128)S(1)}, s32[27,256]{1,0:T(8,128)}, u32[]{:S(2)}) copy-start(s32[27,256]{1,0:T(8,128)} %param.22) | copy-start | bytes 82948
  47.1 14.2 %copy-start.1 = (f32[2,121,121]{2,0,1:T(2,128)S(1)}, f32[2,121,121]{2,0,1:T(2,128)}, u32[]{:S(2)}) copy-start(f32[2,121,121]{2,0,1:T(2,128)} %param.17) | copy-start | bytes 351388
  47.1 14.2 %copy-start.2 = (f32[2,121,121]{2,0,1:T(2,128)S(1)}, f32[2,121,121]{2,0,1:T(2,128)}, u32[]{:S(2)}) copy-start(f32[2,121,121]{2,0,1:T(2,128)} %param.16) | copy-start | bytes 351388
  47.2 1.9 %copy-start.8 = (f32[121,8]{0,1:T(8,128)}, f32[121,8]{0,1:T(8,128)S(1)}, u32[]{:S(2)}) copy-start(f32[121,8]{0,1:T(8,128)S(1)} %slice.62) | copy-start | bytes 11620
  47.2 2.0 %copy-start.9 = (f32[121,8]{0,1:T(8,128)}, f32[121,8]{0,1:T(8,128)S(1)}, u32[]{:S(2)}) copy-start(f32[121,8]{0,1:T(8,128)S(1)} %slice.63) | copy-start | bytes 11620
  47.7 0.6 copy-start.17
  47.7 1.5 copy-start.18
  48.2 1.0 copy-start.19
  48.3 0.9 copy-start.20
  48.7 0.6 copy-start.16
  49.3 14.4 %collective-permute-start = (f32[121,1]{0,1:T(1,128)S(1)}, f32[121,1]{0,1:T(1,128)S(1)}, u32[]{:S(2)}, u32[]{:S(2)}) collective-permute-start(f32[121,1]{0,1:T(1,128)S(1)} %fusion.65), channel_id=1, source_target_pairs={{0,1},{1,0},{2,3},{3,2},{4,5},{5,4},{6,7},{7,6},{8,9},{9,8},{10,11... | collective-permute-start | bytes 1460 | tf_op jit(solution)/shard_map/ppermute | solution.py:40
  50.4 66.7 %collective-permute-start.15 = (bf16[128,32]{0,1:T(8,128)(2,1)}, bf16[128,32]{0,1:T(8,128)(2,1)}, u32[]{:S(2)}, u32[]{:S(2)}) collective-permute-start(bf16[128,32]{0,1:T(8,128)(2,1)} %get-tuple-element.58), channel_id=1, source_target_pairs={{0,1},{1,2},{2,3},{3,4},{4,5},{5,6},{6,7},{7,8},{8,9},{9,10},{10,1... | collective-permute-start | bytes 24584 | tf_op jit(solution)/shard_map/ppermute | solution.py:19
  57.1 5.9 %copy-start.7 = (s32[9,256]{1,0:T(8,128)S(1)}, s32[9,256]{1,0:T(8,128)}, u32[]{:S(2)}) copy-start(s32[9,256]{1,0:T(8,128)} %param.23) | copy-start | bytes 27652
  63.7 11.1 %copy-start.22 = (f32[121,1]{0,1:T(1,128)}, f32[121,1]{0,1:T(1,128)S(1)}, u32[]{:S(2)}) copy-start(f32[121,1]{0,1:T(1,128)S(1)} %collective-permute-done) | copy-start | bytes 1456
  64.1 2.5 %collective-permute-start.1 = (f32[121,1]{0,1:T(1,128)S(1)}, f32[121,1]{0,1:T(1,128)S(1)}, u32[]{:S(2)}, u32[]{:S(2)}) collective-permute-start(f32[121,1]{0,1:T(1,128)S(1)} %fusion.63), channel_id=1, source_target_pairs={{0,2},{2,0},{1,3},{3,1},{4,6},{6,4},{5,7},{7,5},{8,10},{10,8},{9,1... | collective-permute-start | bytes 1460 | tf_op jit(solution)/shard_map/ppermute | solution.py:40
  66.6 8.2 %copy-start.23 = (f32[121,1]{0,1:T(1,128)}, f32[121,1]{0,1:T(1,128)S(1)}, u32[]{:S(2)}) copy-start(f32[121,1]{0,1:T(1,128)S(1)} %collective-permute-done.1) | copy-start | bytes 1456
  67.0 4.0 %collective-permute-start.2 = (f32[121,1]{0,1:T(1,128)S(1)}, f32[121,1]{0,1:T(1,128)S(1)}, u32[]{:S(2)}, u32[]{:S(2)}) collective-permute-start(f32[121,1]{0,1:T(1,128)S(1)} %fusion.61), channel_id=1, source_target_pairs={{0,4},{4,0},{1,5},{5,1},{2,6},{6,2},{3,7},{7,3},{8,12},{12,8},{9,1... | collective-permute-start | bytes 1460 | tf_op jit(solution)/shard_map/ppermute | solution.py:40
  71.0 3.9 %copy-start.24 = (f32[121,1]{0,1:T(1,128)}, f32[121,1]{0,1:T(1,128)S(1)}, u32[]{:S(2)}) copy-start(f32[121,1]{0,1:T(1,128)S(1)} %collective-permute-done.2) | copy-start | bytes 1456
  71.4 2.5 %collective-permute-start.3 = (f32[121,1]{0,1:T(1,128)S(1)}, f32[121,1]{0,1:T(1,128)S(1)}, u32[]{:S(2)}, u32[]{:S(2)}) collective-permute-start(f32[121,1]{0,1:T(1,128)S(1)} %fusion.59), channel_id=1, source_target_pairs={{0,8},{8,0},{1,9},{9,1},{2,10},{10,2},{3,11},{11,3},{4,12},{12,4},... | collective-permute-start | bytes 1460 | tf_op jit(solution)/shard_map/ppermute | solution.py:40
  73.8 1.0 copy-start.25
  74.8 4.2 %collective-permute-start.4 = (f32[121,1]{0,1:T(1,128)}, f32[121,1]{0,1:T(1,128)}, u32[]{:S(2)}, u32[]{:S(2)}) collective-permute-start(f32[121,1]{0,1:T(1,128)} %fusion.57), channel_id=1, source_target_pairs={{0,16},{16,0},{1,17},{17,1},{2,18},{18,2},{3,19},{19,3},{4,20},{20... | collective-permute-start | bytes 1460 | tf_op jit(solution)/shard_map/ppermute | solution.py:40
  80.7 2.5 %collective-permute-start.5 = (f32[121,1]{0,1:T(1,128)S(1)}, f32[121,1]{0,1:T(1,128)S(1)}, u32[]{:S(2)}, u32[]{:S(2)}) collective-permute-start(f32[121,1]{0,1:T(1,128)S(1)} %fusion.55), channel_id=1, source_target_pairs={{0,32},{32,0},{1,33},{33,1},{2,34},{34,2},{3,35},{35,3},{4,36},{36... | collective-permute-start | bytes 1460 | tf_op jit(solution)/shard_map/ppermute | solution.py:40
  83.6 4.1 %collective-permute-start.6 = (f32[121,1]{0,1:T(1,128)S(1)}, f32[121,1]{0,1:T(1,128)S(1)}, u32[]{:S(2)}, u32[]{:S(2)}) collective-permute-start(f32[121,1]{0,1:T(1,128)S(1)} %fusion.53), channel_id=1, source_target_pairs={{0,64},{64,0},{1,65},{65,1},{2,66},{66,2},{3,67},{67,3},{4,68},{68... | collective-permute-start | bytes 1460 | tf_op jit(solution)/shard_map/ppermute | solution.py:40
  87.7 32.5 %collective-permute-start.16 = (bf16[128,32]{0,1:T(8,128)(2,1)}, bf16[128,32]{0,1:T(8,128)(2,1)S(1)}, u32[]{:S(2)}, u32[]{:S(2)}) collective-permute-start(bf16[128,32]{0,1:T(8,128)(2,1)} %get-tuple-element.59), channel_id=1, source_target_pairs={{1,0},{2,1},{3,2},{4,3},{5,4},{6,5},{7,6},{8,7},{9,8},{10,9},{11,1... | collective-permute-start | bytes 24584 | tf_op jit(solution)/shard_map/ppermute | solution.py:22
  113.5 3.7 %copy-start.15 = (bf16[121,128]{0,1:T(8,128)(2,1)S(1)}, bf16[121,128]{0,1:T(8,128)(2,1)}, u32[]{:S(2)}) copy-start(bf16[121,128]{0,1:T(8,128)(2,1)} %select_bitcast_fusion.4) | copy-start | bytes 92932
  113.5 6.7 %copy-start.14 = (bf16[121,128]{0,1:T(8,128)(2,1)S(1)}, bf16[121,128]{0,1:T(8,128)(2,1)}, u32[]{:S(2)}) copy-start(bf16[121,128]{0,1:T(8,128)(2,1)} %select_bitcast_fusion.3) | copy-start | bytes 92932
  117.2 29.2 %collective-permute-start.10 = (bf16[121,128]{0,1:T(8,128)(2,1)S(1)}, bf16[121,128]{0,1:T(8,128)(2,1)S(1)}, u32[]{:S(2)}, u32[]{:S(2)}) collective-permute-start(bf16[121,128]{0,1:T(8,128)(2,1)S(1)} %copy-done.15), channel_id=1, source_target_pairs={{0,1},{1,2},{2,3},{3,4},{4,5},{5,6},{6,7},{7,8},{8,9},{9,10},{10,1... | collective-permute-start | bytes 92936 | tf_op jit(solution)/shard_map/ppermute | solution.py:30
  120.2 26.2 %collective-permute-start.11 = (bf16[121,128]{0,1:T(8,128)(2,1)S(1)}, bf16[121,128]{0,1:T(8,128)(2,1)S(1)}, u32[]{:S(2)}, u32[]{:S(2)}) collective-permute-start(bf16[121,128]{0,1:T(8,128)(2,1)S(1)} %copy-done.14), channel_id=1, source_target_pairs={{1,0},{2,1},{3,2},{4,3},{5,4},{6,5},{7,6},{8,7},{9,8},{10,9},{11,1... | collective-permute-start | bytes 92936 | tf_op jit(solution)/shard_map/ppermute | solution.py:30
  122.8 4.7 %copy-start.26 = (pred[9,256]{1,0:T(8,128)(4,1)S(1)}, pred[9,256]{1,0:T(8,128)(4,1)}, u32[]{:S(2)}) copy-start(pred[9,256]{1,0:T(8,128)(4,1)} %compare_and_fusion.2) | copy-start | bytes 6916
  127.5 1.5 copy-start.13
  127.5 9.3 %copy-start.12 = (bf16[121,128]{0,1:T(8,128)(2,1)S(1)}, bf16[121,128]{0,1:T(8,128)(2,1)}, u32[]{:S(2)}) copy-start(bf16[121,128]{0,1:T(8,128)(2,1)} %select_bitcast_fusion.1) | copy-start | bytes 92932
  127.5 13.9 %copy-start.11 = (bf16[121,128]{0,1:T(8,128)(2,1)S(1)}, bf16[121,128]{0,1:T(8,128)(2,1)}, u32[]{:S(2)}) copy-start(bf16[121,128]{0,1:T(8,128)(2,1)} %select_bitcast_fusion) | copy-start | bytes 92932
  129.0 20.5 %copy-start.6 = (s32[7168]{0:T(1024)S(1)}, s32[7168]{0:T(1024)}, u32[]{:S(2)}) copy-start(s32[7168]{0:T(1024)} %pad_clamp_fusion) | copy-start | bytes 86020
  129.0 17.4 %collective-permute-start.12 = (bf16[121,128]{0,1:T(8,128)(2,1)S(1)}, bf16[121,128]{0,1:T(8,128)(2,1)S(1)}, u32[]{:S(2)}, u32[]{:S(2)}) collective-permute-start(bf16[121,128]{0,1:T(8,128)(2,1)S(1)} %copy-done.13), channel_id=1, source_target_pairs={{2,0},{3,1},{4,2},{5,3},{6,4},{7,5},{8,6},{9,7},{10,8},{11,9},{12,... | collective-permute-start | bytes 92936 | tf_op jit(solution)/shard_map/ppermute | solution.py:30
  136.8 9.6 %collective-permute-start.13 = (bf16[121,128]{0,1:T(8,128)(2,1)S(1)}, bf16[121,128]{0,1:T(8,128)(2,1)S(1)}, u32[]{:S(2)}, u32[]{:S(2)}) collective-permute-start(bf16[121,128]{0,1:T(8,128)(2,1)S(1)} %copy-done.12), channel_id=1, source_target_pairs={{3,0},{4,1},{5,2},{6,3},{7,4},{8,5},{9,6},{10,7},{11,8},{12,9},{13... | collective-permute-start | bytes 92936 | tf_op jit(solution)/shard_map/ppermute | solution.py:30
  141.4 6.7 %collective-permute-start.14 = (bf16[121,128]{0,1:T(8,128)(2,1)S(1)}, bf16[121,128]{0,1:T(8,128)(2,1)S(1)}, u32[]{:S(2)}, u32[]{:S(2)}) collective-permute-start(bf16[121,128]{0,1:T(8,128)(2,1)S(1)} %copy-done.11), channel_id=1, source_target_pairs={{4,0},{5,1},{6,2},{7,3},{8,4},{9,5},{10,6},{11,7},{12,8},{13,9},{1... | collective-permute-start | bytes 92936 | tf_op jit(solution)/shard_map/ppermute | solution.py:30
  149.6 14.8 %copy-start.21 = (pred[27,256]{1,0:T(8,128)(4,1)S(1)}, pred[27,256]{1,0:T(8,128)(4,1)}, u32[]{:S(2)}) copy-start(pred[27,256]{1,0:T(8,128)(4,1)} %get-tuple-element.6) | copy-start | bytes 20740
  149.6 14.8 %copy-start.27 = (bf16[128,121]{1,0:T(8,128)(2,1)S(1)}, bf16[128,121]{1,0:T(8,128)(2,1)}, u32[]{:S(2)}) copy-start(bf16[128,121]{1,0:T(8,128)(2,1)} %param.19) | copy-start | bytes 92932
where the time goes:
time: 169 us; the launch traced here: 168 us
  starting transfers between devices  64.2 us (38%)
  local copies, waits for them, and re-layouts  47.7 us (28%)
  matrix products  34.2 us (20%)
  other arithmetic  14.1 us (8%)
  waiting for transfers between devices  6.72 us (4%)
    ppermute x8, starting transfers between devices, shifted(): return lax.ppermute(shard, axis, pairs)  32.1 us
    gather x1, local copies, waits for them, and re-layouts, body(): jnp.take(sources, mapped.reshape(-1), axis=1)  14.8 us
    gather x1, local copies, waits for them, and re-layouts, body(): jnp.take(multipole, far_cells, axis=1)  12.1 us
    ppermute x7, starting transfers between devices, swapped(): return lax.ppermute(block, axis, route)  10.9 us
    all_to_all x1, starting transfers between devices, body(): lax.all_to_all(jnp.take(multipole, far_cells, axis=1), 'leaf', split_axis...  9.91 us
    ppermute x1, starting transfers between devices, with_halo(): lax.ppermute(lax.slice_in_dim(block, 0, width, axis=dim), axis, backward)  8.19 us
    dot_general x7, matrix products, body(): jnp.dot(far_pick, siblings[tree_bit], precision=precise)  6.35 us
    gather x8, local copies, waits for them, and re-layouts, body(): pieces.append(shifted(jnp.take(multipole, chosen, axis=1), 'leaf', -offset))  5.69 us
  transfers between devices with their start and end apart: 18, of which 7 were waited for; matrix products, arithmetic and copies ran while one was open for 43% of the time, Pallas kernels for 0%

commit v1 on v0

v1 whole, which is shorter than its diff:
```python
import functools

import jax
import jax.numpy as jnp
from jax import lax
from jax.experimental import pallas as pl
from jax.experimental.pallas import tpu as pltpu
from jax.sharding import PartitionSpec as P

N = 128
CELLS = 256
COEF = 121
FAR = 32
NEARCAP = 128
HALO = 32
FIRST = 5
LAST = 123
f32 = jnp.float32
bf16 = jnp.bfloat16
MESH = pl.DeviceIdType.MESH
NT = (((1,), (1,)), ((), ()))
TN = (((0,), (0,)), ((), ()))


def exchange(slip_ref, wm_ref, send_ref, mt_ref, near_ref, far_ref, halo_ref,
             wp, sendbuf, nearbuf, halobuf, send_sem, far_sem, near_sem, halo_sem):
    me = lax.axis_index("leaf")
    barrier = pltpu.get_barrier_semaphore()

    def hello(k, carry):
        pl.semaphore_signal(barrier, inc=1, device_id=(lax.rem(me + k, N),), device_id_type=MESH)
        return carry

    lax.fori_loop(1, N, hello, 0)
    wp[...] = jnp.zeros_like(wp)
    wp[0:COEF, :] = wm_ref[...]
    mt = lax.dot_general(slip_ref[...], wp[...], (((0,), (1,)), ((), ())), preferred_element_type=f32).astype(bf16)
    mt_ref[...] = mt
    cell = lax.broadcasted_iota(jnp.int32, (HALO, CELLS), 1)
    row = lax.broadcasted_iota(jnp.int32, (HALO, CELLS), 0)
    for side in range(2):
        pick = (cell == row + (CELLS - HALO) * (1 - side)).astype(f32).astype(bf16)
        halobuf[side] = lax.dot_general(pick, slip_ref[...], NT, preferred_element_type=f32).astype(bf16)
    lists = pltpu.roll(send_ref[...].astype(f32).T, lax.rem(N - me, N), 1)
    lane = lax.broadcasted_iota(jnp.int32, (NEARCAP, CELLS), 1).astype(f32)
    near_at = (1, 2, 3, 4, 124, 125, 126, 127)
    for i, k in enumerate(near_at):
        hot = (lists[:, k:k + 1] == lane).astype(f32).astype(bf16)
        nearbuf[i] = jnp.dot(hot, mt, preferred_element_type=f32).astype(bf16)
    for k in range(FIRST, LAST + 1):
        hot = (lists[0:FAR, k:k + 1] == lane[0:FAR]).astype(f32).astype(bf16)
        sendbuf[k] = jnp.dot(hot, mt, preferred_element_type=f32).astype(bf16)
    pl.semaphore_wait(barrier, N - 1)

    def far_copy(k):
        return pltpu.make_async_remote_copy(
            src_ref=sendbuf.at[k], dst_ref=far_ref.at[me], send_sem=send_sem.at[0], recv_sem=far_sem,
            device_id=(lax.rem(me + k, N),), device_id_type=MESH)

    def near_copy(i, k):
        return pltpu.make_async_remote_copy(
            src_ref=nearbuf.at[i], dst_ref=near_ref.at[i], send_sem=send_sem.at[1], recv_sem=near_sem,
            device_id=(lax.rem(me + k, N),), device_id_type=MESH)

    def halo_copy(side):
        return pltpu.make_async_remote_copy(
            src_ref=halobuf.at[side], dst_ref=halo_ref.at[side], send_sem=send_sem.at[2], recv_sem=halo_sem,
            device_id=(lax.rem(me + (1, N - 1)[side], N),), device_id_type=MESH)

    for side in range(2):
        halo_copy(side).start()
    for i, k in enumerate(near_at):
        near_copy(i, k).start()

    def go(i, carry):
        far_copy(FIRST + lax.rem(i * 37, LAST - FIRST + 1)).start()
        return carry

    lax.fori_loop(0, LAST - FIRST + 1, go, 0)
    count = LAST - FIRST + 1
    pltpu.make_async_copy(halobuf, halobuf, send_sem.at[2]).wait()
    pltpu.make_async_copy(halobuf, halo_ref, halo_sem).wait()
    pltpu.make_async_copy(nearbuf, nearbuf, send_sem.at[1]).wait()
    pltpu.make_async_copy(nearbuf, near_ref, near_sem).wait()
    pltpu.make_async_copy(sendbuf.at[0:count], sendbuf.at[0:count], send_sem.at[0]).wait()
    pltpu.make_async_copy(sendbuf.at[0:count], sendbuf.at[0:count], far_sem).wait()


def call_exchange(slip, to_multipole, send):
    vm = pl.BlockSpec(memory_space=pltpu.VMEM)
    return pl.pallas_call(
        exchange,
        out_shape=(
            jax.ShapeDtypeStruct((CELLS, 128), bf16),
            jax.ShapeDtypeStruct((8, NEARCAP, 128), bf16),
            jax.ShapeDtypeStruct((N, FAR, 128), bf16),
            jax.ShapeDtypeStruct((2, HALO, 128), bf16),
        ),
        in_specs=[vm] * 3,
        out_specs=(vm,) * 4,
        scratch_shapes=[
            pltpu.VMEM((128, 128), bf16),
            pltpu.VMEM((N, FAR, 128), bf16),
            pltpu.VMEM((8, NEARCAP, 128), bf16),
            pltpu.VMEM((2, HALO, 128), bf16),
            pltpu.SemaphoreType.DMA((3,)),
            pltpu.SemaphoreType.DMA,
            pltpu.SemaphoreType.DMA,
            pltpu.SemaphoreType.DMA,
        ],
        compiler_params=pltpu.CompilerParams(collective_id=0, has_side_effects=True),
        name="exchange",
    )(slip, to_multipole, send.reshape(N, NEARCAP))


def swapped(block, axis, stride):
    count = lax.axis_size(axis)
    route = []
    for low in range(count):
        high = low | 1 << stride
        if high != low and high < count:
            route += [(low, high), (high, low)]
    return lax.ppermute(block, axis, route)


def pair_up(up_shift, lower, upper):
    precise = lax.Precision.HIGHEST
    return jnp.dot(up_shift[0], lower, precision=precise) + jnp.dot(up_shift[1], upper, precision=precise)


def body(slip, to_multipole, up_shift, down_shift, sibling_far, leaf_far, to_stress, near_blocks,
         send_cells, far_list, near_list):
    precise = lax.Precision.HIGHEST
    me = lax.axis_index("leaf")
    mt, near_rows, far_rows, halos = call_exchange(slip, to_multipole, send_cells)
    multipole = mt[:, :COEF].T
    left = jnp.where(me > 0, halos[0].T, 0)
    right = jnp.where(me < N - 1, halos[1].T, 0)
    extended = jnp.concatenate([left, slip, right], axis=1)
    near_cols = jnp.take(extended, near_list.reshape(-1), axis=1, mode="clip").reshape(128, 9, CELLS)
    near_part = jnp.einsum("kij,jkc->ic", near_blocks, near_cols, preferred_element_type=f32)
    table = jnp.concatenate([mt, near_rows.reshape(-1, 128), far_rows.reshape(-1, 128)], axis=0)
    rel = far_list - CELLS
    sender = rel // NEARCAP
    slot = rel % NEARCAP
    off = (me - sender) % N
    near_i = jnp.where(off <= 4, off - 1, off - 120)
    is_near = (off <= 4) | (off >= 124)
    row = jnp.where(far_list < CELLS, far_list,
                    jnp.where(is_near, CELLS + near_i * NEARCAP + slot, CELLS + 8 * NEARCAP + sender * FAR + slot))
    cols = jnp.take(table, row.reshape(-1), axis=0, mode="clip").reshape(27, CELLS, 128)[:, :, :COEF]
    leaf_sum = jnp.einsum("tij,tcj->ic", leaf_far, cols, preferred_element_type=f32)
    aggregates = [multipole.astype(f32)]
    for height in range(8):
        below = aggregates[-1]
        aggregates.append(pair_up(up_shift, below[:, 0::2], below[:, 1::2]))
    current = aggregates[-1]
    siblings = []
    for bit in range(7):
        partner = swapped(current, "leaf", bit)
        siblings.append(partner)
        if bit < 6:
            branch = me >> bit & 1
            current = pair_up(up_shift, jnp.where(branch == 0, current, partner),
                              jnp.where(branch == 0, partner, current))
    expansion = jnp.zeros((COEF, 1), f32)
    for bit in reversed(range(7)):
        branch = me >> bit & 1
        down_pick = lax.dynamic_index_in_dim(down_shift, branch, 0, keepdims=False)
        far_pick = lax.dynamic_index_in_dim(sibling_far, branch, 0, keepdims=False)
        expansion = jnp.dot(down_pick, expansion, precision=precise) + jnp.dot(far_pick, siblings[bit], precision=precise)
    for height in reversed(range(8)):
        a = jnp.dot(down_shift[0], expansion, precision=precise)
        b = jnp.dot(down_shift[1], expansion, precision=precise)
        if height >= 1:
            sums = aggregates[height]
            a = a + jnp.dot(sibling_far[0], sums[:, 1::2], precision=precise)
            b = b + jnp.dot(sibling_far[1], sums[:, 0::2], precision=precise)
        expansion = jnp.stack([a, b], axis=-1).reshape(COEF, -1)
    local_exp = (expansion + leaf_sum).astype(bf16)
    return jnp.dot(to_stress, local_exp, preferred_element_type=f32) + near_part


def solution(mesh):
    cut = P(None, "leaf")
    return jax.shard_map(body, mesh=mesh,
                         in_specs=(cut, P(), P(), P(), P(), P(), P(), P(), P("leaf", None), cut, cut),
                         out_specs=cut, check_vma=False)
```

time: 169 us -> 93.6 us (0.55)
  the two profiles are of different devices: /device:TPU:7 before, /device:TPU:0 now
where the time goes in v1:
time: 93.6 us; the launch traced here: 93.3 us
  Pallas kernels  29 us (31%)
  local copies, waits for them, and re-layouts  25.2 us (27%)
  matrix products  19.8 us (21%)
  waiting for transfers between devices  8.4 us (9%)
  starting transfers between devices  8.31 us (9%)
  other arithmetic  1.56 us (2%)
  between operations  1.07 us (1%)
    pallas_call x1, Pallas kernels, call_exchange(): pl.pallas_call(exchange, out_shape=(jax.ShapeDtypeStruct((CELLS, 128), bf...  29 us
    gather x1, local copies, waits for them, and re-layouts, body(): jnp.take(table, row.reshape(-1), axis=0, mode='clip')  14.7 us
    ppermute x7, waiting for transfers between devices, swapped(): return lax.ppermute(block, axis, route)  8.4 us
    ppermute x7, starting transfers between devices, swapped(): return lax.ppermute(block, axis, route)  8.31 us
    gather x1, local copies, waits for them, and re-layouts, body(): jnp.take(extended, near_list.reshape(-1), axis=1, mode='clip')  4.67 us
    dot_general x14, matrix products, pair_up(): jnp.dot(up_shift[0], lower, precision=precise)  3.5 us
    dot_general x14, matrix products, pair_up(): jnp.dot(up_shift[1], upper, precision=precise)  2.79 us
    dot_general x7, matrix products, body(): jnp.dot(down_pick, expansion, precision=precise)  2.14 us
  transfers between devices with their start and end apart: 7, of which 4 were waited for; matrix products, arithmetic and copies ran while one was open for 27% of the time, Pallas kernels for 0%

profile of v1, /device:TPU:0, one launch (start us, length us, event | category | flops | bytes accessed | tf_op | source)
XLA Modules:
  0.0 93.3 jit_solution(11194980916529339218)
XLA Ops:
  0.0 29.0 %exchange.1 = (bf16[256,128]{1,0:T(8,128)(2,1)}, bf16[8,128,128]{2,1,0:T(8,128)(2,1)}, bf16[128,32,128]{2,1,0:T(8,128)(2,1)}, bf16[2,32,128]{2,1,0:T(8,128)(2,1)}) custom-call(bf16[128,256]{1,0:T(8,128)(2,1)} %slip_ref.1, bf16[121,128]{1,0:T(8,128)(2,1)} %wm_ref.1, s32[128,128]{1,0:T(8,128)} %bitcast.476), custom_call_target="tpu_custom_call" | custom-call | tf_op jit(solution)/shard_map/exchange/pallas_call | solution.py:91
  29.0 0.9 slice_bitcast_fusion
  30.0 1.1 %fusion.97 = (f32[1,121,121]{2,0,1:T(1,128)S(1)}, f32[1,121,121]{2,0,1:T(1,128)S(1)}) fusion(f32[2,121,121]{2,0,1:T(2,128)} %param.13), kind=kLoop, calls=%fused_computation.217 | loop fusion | bytes 234256 | tf_op jit(solution)/shard_map/slice | solution.py:128
  31.6 0.2 fusion.82
  31.8 0.2 fusion.17
  32.3 0.2 fusion.20
  33.3 0.2 fusion.26
  33.8 0.2 fusion.29
  34.3 0.2 fusion.32
  34.6 0.2 convolution_bitcast_fusion.33
  34.8 0.2 fusion.64
  35.2 1.3 %pad_maximum_fusion = bf16[5376,128]{1,0:T(8,128)(2,1)S(1)} fusion(bf16[4096,128]{1,0:T(8,128)(2,1)} %bitcast.465, bf16[1024,128]{1,0:T(8,128)(2,1)S(1)} %bitcast.471, bf16[256,128]{1,0:T(8,128)(2,1)S(1)} %copy-done.21), kind=kLoop, calls=%fused_computation.4 | loop fusion | flops 4128768 | bytes 2752512 | tf_op jit(solution)/shard_map/concatenate | solution.py:142
  36.6 1.8 %fusion.95 = (f32[1,121,121]{2,0,1:T(1,128)S(1)}, f32[1,121,121]{2,0,1:T(1,128)}, f32[1,121,121]{2,0,1:T(1,128)}, f32[1,121,121]{2,0,1:T(1,128)}, f32[1,121,121]...) fusion(f32[2,121,121]{2,0,1:T(2,128)S(1)} %copy-done.2, ...), kind=kLoop, calls=%fused_computation.215 | loop fusion | bytes 2108332 | tf_op jit(solution)/shard_map/slice | solution.py:177
  38.6 0.2 fusion.62
  38.9 0.8 collective-permute-start.1
  39.8 2.7 %collective-permute-done.1 = f32[121,1]{0,1:T(1,128)S(1)} collective-permute-done((f32[121,1]{0,1:T(1,128)S(1)}, f32[121,1]{0,1:T(1,128)S(1)}, u32[]{:S(2)}, u32[]{:S(2)}) %collective-permute-start.1) | collective-permute-done | bytes 516 | tf_op jit(solution)/shard_map/ppermute | solution.py:123
  42.7 0.2 fusion.60
  42.9 1.7 %collective-permute-start.2 = (f32[121,1]{0,1:T(1,128)S(1)}, f32[121,1]{0,1:T(1,128)S(1)}, u32[]{:S(2)}, u32[]{:S(2)}) collective-permute-start(f32[121,1]{0,1:T(1,128)S(1)} %fusion.60), channel_id=1, source_target_pairs={{0,4},{4,0},{1,5},{5,1},{2,6},{6,2},{3,7},{7,3},{8,12},{12,8},{9,1... | collective-permute-start | bytes 1460 | tf_op jit(solution)/shard_map/ppermute | solution.py:123
  44.6 3.4 %collective-permute-done.2 = f32[121,1]{0,1:T(1,128)S(1)} collective-permute-done((f32[121,1]{0,1:T(1,128)S(1)}, f32[121,1]{0,1:T(1,128)S(1)}, u32[]{:S(2)}, u32[]{:S(2)}) %collective-permute-start.2) | collective-permute-done | bytes 516 | tf_op jit(solution)/shard_map/ppermute | solution.py:123
  48.2 0.2 fusion.58
  48.4 0.5 collective-permute-start.3
  48.9 4.7 %gather_fusion.1 = bf16[2304,128]{1,0:T(8,128)(2,1)S(1)} fusion(bf16[128,320]{0,1:T(8,128)(2,1)S(1)} %pad_maximum_fusion.2, s32[3072]{0:T(1024)S(1)} %pad_clamp_fusion.1), kind=kCustom, calls=%fused_computation.1 | custom fusion | bytes 1188864 | tf_op jit(solution)/shard_map/jit(_take)/gather | solution.py:140
  53.8 0.2 fusion.56
  54.0 2.9 %collective-permute-start.4 = (f32[121,1]{0,1:T(1,128)S(1)}, f32[121,1]{0,1:T(1,128)S(1)}, u32[]{:S(2)}, u32[]{:S(2)}) collective-permute-start(f32[121,1]{0,1:T(1,128)S(1)} %fusion.56), channel_id=1, source_target_pairs={{0,16},{16,0},{1,17},{17,1},{2,18},{18,2},{3,19},{19,3},{4,20},{20... | collective-permute-start | bytes 1460 | tf_op jit(solution)/shard_map/ppermute | solution.py:123
  56.9 1.9 %convolution_bitcast_fusion = f32[256,128]{1,0:T(8,128)} fusion(bf16[128,9,256]{0,2,1:T(8,128)(2,1)S(1)} %bitcast.464, bf16[9,128,128]{2,1,0:T(8,128)(2,1)} %param.18), kind=kOutput, calls=%fused_computation.6 | convolution fusion | flops 75497472 | bytes 1015808 | tf_op jit(solution)/shard_map/kij,jkc->ic/dot_general | solution.py:141
  58.9 0.3 collective-permute-done.4
  59.3 0.2 fusion.54
  59.6 0.8 collective-permute-start.5
  60.4 0.8 convolution_bitcast_fusion.34
  61.2 2.0 %collective-permute-done.5 = f32[121,1]{0,1:T(1,128)S(1)} collective-permute-done((f32[121,1]{0,1:T(1,128)S(1)}, f32[121,1]{0,1:T(1,128)S(1)}, u32[]{:S(2)}, u32[]{:S(2)}) %collective-permute-start.5) | collective-permute-done | bytes 516 | tf_op jit(solution)/shard_map/ppermute | solution.py:123
  63.4 0.8 fusion.52
  64.2 1.6 %collective-permute-start.6 = (f32[121,1]{0,1:T(1,128)}, f32[121,1]{0,1:T(1,128)}, u32[]{:S(2)}, u32[]{:S(2)}) collective-permute-start(f32[121,1]{0,1:T(1,128)} %fusion.52), channel_id=1, source_target_pairs={{0,64},{64,0},{1,65},{65,1},{2,66},{66,2},{3,67},{67,3},{4,68},{68... | collective-permute-start | bytes 1460 | tf_op jit(solution)/shard_map/ppermute | solution.py:123
  66.0 14.7 %gather_fusion = bf16[6912,128]{1,0:T(8,128)(2,1)} fusion(bf16[5376,128]{1,0:T(8,128)(2,1)S(1)} %pad_maximum_fusion, s32[7168]{0:T(1024)S(1)} %pad_clamp_fusion), kind=kCustom, calls=%fused_computation | custom fusion | bytes 3566592 | tf_op jit(solution)/shard_map/jit(_take)/gather | solution.py:151
  80.8 0.8 fusion.50
  81.6 0.2 convolution_bitcast_fusion.18
  82.1 0.2 convolution_bitcast_fusion.16
  82.6 0.2 convolution_bitcast_fusion.14
  83.0 0.2 convolution_bitcast_fusion.12
  83.5 0.2 convolution_bitcast_fusion.10
  83.9 0.2 convolution_bitcast_fusion.8
  84.4 0.2 convolution_bitcast_fusion.6
  84.6 0.2 convolution_bitcast_fusion.4
  84.8 0.2 fusion.36
  85.1 0.2 fusion.34
  85.3 0.2 fusion.70
  85.5 0.2 fusion.76
  86.0 0.2 fusion.30
  86.5 0.2 fusion.75
  86.7 0.2 fusion.28
  86.9 0.2 fusion.27
  87.4 0.2 fusion.74
  87.6 0.2 fusion.25
  87.8 0.2 fusion.24
  88.3 0.2 fusion.73
  88.8 0.2 fusion.21
  89.5 0.2 fusion.19
  90.0 0.2 fusion.65
  90.3 0.2 fusion.71
  90.5 0.2 fusion.16
  90.8 0.2 fusion.15
  91.1 0.3 convolution_bitcast_fusion.2
  91.4 0.3 convolution_bitcast_fusion.1
  91.8 0.8 fusion.5
  92.6 0.8 copy.42
  (186 shorter events, 6.9 us)
Async XLA Ops:
  0.0 91.8 %copy-start = (bf16[27,121,121]{2,1,0:T(8,128)(2,1)S(1)}, bf16[27,121,121]{2,1,0:T(8,128)(2,1)}, u32[]{:S(2)}) copy-start(bf16[27,121,121]{2,1,0:T(8,128)(2,1)} %param.16) | copy-start | bytes 2371846
  29.0 6.2 %copy-start.21 = (bf16[256,128]{1,0:T(8,128)(2,1)S(1)}, bf16[256,128]{1,0:T(8,128)(2,1)}, u32[]{:S(2)}) copy-start(bf16[256,128]{1,0:T(8,128)(2,1)} %get-tuple-element.9) | copy-start | bytes 196612
  29.0 6.2 %copy-start.23 = (bf16[8,128,128]{2,1,0:T(8,128)(2,1)S(1)}, bf16[8,128,128]{2,1,0:T(8,128)(2,1)}, u32[]{:S(2)}) copy-start(bf16[8,128,128]{2,1,0:T(8,128)(2,1)} %get-tuple-element.10) | copy-start | bytes 786436
  31.5 3.5 %copy-start.5 = (f32[121,64]{0,1:T(8,128)}, f32[121,64]{0,1:T(8,128)S(1)}, u32[]{:S(2)}) copy-start(f32[121,64]{0,1:T(8,128)S(1)} %slice.59) | copy-start | bytes 92932
  32.1 3.0 %copy-start.24 = (f32[121,32]{0,1:T(8,128)}, f32[121,32]{0,1:T(8,128)S(1)}, u32[]{:S(2)}) copy-start(f32[121,32]{0,1:T(8,128)S(1)} %slice.61) | copy-start | bytes 46468
  32.6 2.5 %copy-start.26 = (f32[121,16]{0,1:T(8,128)}, f32[121,16]{0,1:T(8,128)S(1)}, u32[]{:S(2)}) copy-start(f32[121,16]{0,1:T(8,128)S(1)} %slice.64) | copy-start | bytes 23236
  32.8 3.7 %copy-start.2 = (f32[2,121,121]{2,0,1:T(2,128)S(1)}, f32[2,121,121]{2,0,1:T(2,128)}, u32[]{:S(2)}) copy-start(f32[2,121,121]{2,0,1:T(2,128)} %param.15) | copy-start | bytes 351388
  32.8 3.7 %copy-start.3 = (f32[2,121,121]{2,0,1:T(2,128)S(1)}, f32[2,121,121]{2,0,1:T(2,128)}, u32[]{:S(2)}) copy-start(f32[2,121,121]{2,0,1:T(2,128)} %param.14) | copy-start | bytes 351388
  33.1 2.0 %copy-start.28 = (f32[121,8]{0,1:T(8,128)}, f32[121,8]{0,1:T(8,128)S(1)}, u32[]{:S(2)}) copy-start(f32[121,8]{0,1:T(8,128)S(1)} %slice.65) | copy-start | bytes 11620
  33.1 2.0 %copy-start.30 = (f32[121,8]{0,1:T(8,128)}, f32[121,8]{0,1:T(8,128)S(1)}, u32[]{:S(2)}) copy-start(f32[121,8]{0,1:T(8,128)S(1)} %slice.66) | copy-start | bytes 11620
  33.6 1.5 %copy-start.38 = (f32[121,4]{0,1:T(4,128)}, f32[121,4]{0,1:T(4,128)S(1)}, u32[]{:S(2)}) copy-start(f32[121,4]{0,1:T(4,128)S(1)} %slice.68) | copy-start | bytes 5812
  34.1 1.1 %copy-start.42 = (f32[121,2]{0,1:T(2,128)}, f32[121,2]{0,1:T(2,128)S(1)}, u32[]{:S(2)}) copy-start(f32[121,2]{0,1:T(2,128)S(1)} %slice.69) | copy-start | bytes 2908
  34.2 1.0 %copy-start.44 = (f32[121,2]{0,1:T(2,128)}, f32[121,2]{0,1:T(2,128)S(1)}, u32[]{:S(2)}) copy-start(f32[121,2]{0,1:T(2,128)S(1)} %slice.70) | copy-start | bytes 2908
  35.0 3.4 %collective-permute-start = (f32[121,1]{0,1:T(1,128)S(1)}, f32[121,1]{0,1:T(1,128)S(1)}, u32[]{:S(2)}, u32[]{:S(2)}) collective-permute-start(f32[121,1]{0,1:T(1,128)S(1)} %fusion.64), channel_id=1, source_target_pairs={{0,1},{1,0},{2,3},{3,2},{4,5},{5,4},{6,7},{7,6},{8,9},{9,8},{10,11... | collective-permute-start | bytes 1460 | tf_op jit(solution)/shard_map/ppermute | solution.py:123
  36.5 1.9 %copy-start.33 = (s32[27,256]{1,0:T(8,128)S(1)}, s32[27,256]{1,0:T(8,128)}, u32[]{:S(2)}) copy-start(s32[27,256]{1,0:T(8,128)} %param.20) | copy-start | bytes 82948
  36.5 3.1 %copy-start.41 = (bf16[2,32,128]{2,1,0:T(8,128)(2,1)S(1)}, bf16[2,32,128]{2,1,0:T(8,128)(2,1)}, u32[]{:S(2)}) copy-start(bf16[2,32,128]{2,1,0:T(8,128)(2,1)} %get-tuple-element.12) | copy-start | bytes 49156
  36.5 3.1 %copy-start.22 = (bf16[128,256]{1,0:T(8,128)(2,1)S(1)}, bf16[128,256]{1,0:T(8,128)(2,1)}, u32[]{:S(2)}) copy-start(bf16[128,256]{1,0:T(8,128)(2,1)} %slip_ref.1) | copy-start | bytes 196612
  36.5 8.1 %copy-start.40 = (s32[9,256]{1,0:T(8,128)S(1)}, s32[9,256]{1,0:T(8,128)}, u32[]{:S(2)}) copy-start(s32[9,256]{1,0:T(8,128)} %param.21) | copy-start | bytes 27652
  38.5 10.4 %copy-start.46 = (f32[121,1]{0,1:T(1,128)}, f32[121,1]{0,1:T(1,128)S(1)}, u32[]{:S(2)}) copy-start(f32[121,1]{0,1:T(1,128)S(1)} %collective-permute-done) | copy-start | bytes 1456
  38.9 3.6 %collective-permute-start.1 = (f32[121,1]{0,1:T(1,128)S(1)}, f32[121,1]{0,1:T(1,128)S(1)}, u32[]{:S(2)}, u32[]{:S(2)}) collective-permute-start(f32[121,1]{0,1:T(1,128)S(1)} %fusion.62), channel_id=1, source_target_pairs={{0,2},{2,0},{1,3},{3,1},{4,6},{6,4},{5,7},{7,5},{8,10},{10,8},{9,1... | collective-permute-start | bytes 1460 | tf_op jit(solution)/shard_map/ppermute | solution.py:123
  42.5 6.4 %copy-start.48 = (f32[121,1]{0,1:T(1,128)}, f32[121,1]{0,1:T(1,128)S(1)}, u32[]{:S(2)}) copy-start(f32[121,1]{0,1:T(1,128)S(1)} %collective-permute-done.1) | copy-start | bytes 1456
  42.9 5.1 %collective-permute-start.2 = (f32[121,1]{0,1:T(1,128)S(1)}, f32[121,1]{0,1:T(1,128)S(1)}, u32[]{:S(2)}, u32[]{:S(2)}) collective-permute-start(f32[121,1]{0,1:T(1,128)S(1)} %fusion.60), channel_id=1, source_target_pairs={{0,4},{4,0},{1,5},{5,1},{2,6},{6,2},{3,7},{7,3},{8,12},{12,8},{9,1... | collective-permute-start | bytes 1460 | tf_op jit(solution)/shard_map/ppermute | solution.py:123
  48.0 0.9 copy-start.50
  48.4 5.2 %collective-permute-start.3 = (f32[121,1]{0,1:T(1,128)S(1)}, f32[121,1]{0,1:T(1,128)S(1)}, u32[]{:S(2)}, u32[]{:S(2)}) collective-permute-start(f32[121,1]{0,1:T(1,128)S(1)} %fusion.58), channel_id=1, source_target_pairs={{0,8},{8,0},{1,9},{9,1},{2,10},{10,2},{3,11},{11,3},{4,12},{12,4},... | collective-permute-start | bytes 1460 | tf_op jit(solution)/shard_map/ppermute | solution.py:123
  48.9 11.5 %copy-start.20 = (f32[1,121,121]{2,0,1:T(1,128)S(1)}, f32[1,121,121]{2,0,1:T(1,128)}, u32[]{:S(2)}) copy-start(f32[1,121,121]{2,0,1:T(1,128)} %get-tuple-element.42) | copy-start | bytes 175696
  53.6 10.5 %copy-start.52 = (f32[121,1]{0,1:T(1,128)}, f32[121,1]{0,1:T(1,128)S(1)}, u32[]{:S(2)}) copy-start(f32[121,1]{0,1:T(1,128)S(1)} %collective-permute-done.3) | copy-start | bytes 1456
  54.0 5.1 %collective-permute-start.4 = (f32[121,1]{0,1:T(1,128)S(1)}, f32[121,1]{0,1:T(1,128)S(1)}, u32[]{:S(2)}, u32[]{:S(2)}) collective-permute-start(f32[121,1]{0,1:T(1,128)S(1)} %fusion.56), channel_id=1, source_target_pairs={{0,16},{16,0},{1,17},{17,1},{2,18},{18,2},{3,19},{19,3},{4,20},{20... | collective-permute-start | bytes 1460 | tf_op jit(solution)/shard_map/ppermute | solution.py:123
  59.2 6.6 %copy-start.54 = (f32[121,1]{0,1:T(1,128)}, f32[121,1]{0,1:T(1,128)S(1)}, u32[]{:S(2)}) copy-start(f32[121,1]{0,1:T(1,128)S(1)} %collective-permute-done.4) | copy-start | bytes 1456
  59.6 3.6 %collective-permute-start.5 = (f32[121,1]{0,1:T(1,128)S(1)}, f32[121,1]{0,1:T(1,128)S(1)}, u32[]{:S(2)}, u32[]{:S(2)}) collective-permute-start(f32[121,1]{0,1:T(1,128)S(1)} %fusion.54), channel_id=1, source_target_pairs={{0,32},{32,0},{1,33},{33,1},{2,34},{34,2},{3,35},{35,3},{4,36},{36... | collective-permute-start | bytes 1460 | tf_op jit(solution)/shard_map/ppermute | solution.py:123
  63.2 1.0 %copy-start.56 = (f32[121,1]{0,1:T(1,128)}, f32[121,1]{0,1:T(1,128)S(1)}, u32[]{:S(2)}) copy-start(f32[121,1]{0,1:T(1,128)S(1)} %collective-permute-done.5) | copy-start | bytes 1456
  64.2 16.6 %collective-permute-start.6 = (f32[121,1]{0,1:T(1,128)}, f32[121,1]{0,1:T(1,128)}, u32[]{:S(2)}, u32[]{:S(2)}) collective-permute-start(f32[121,1]{0,1:T(1,128)} %fusion.52), channel_id=1, source_target_pairs={{0,64},{64,0},{1,65},{65,1},{2,66},{66,2},{3,67},{67,3},{4,68},{68... | collective-permute-start | bytes 1460 | tf_op jit(solution)/shard_map/ppermute | solution.py:123
  65.8 15.0 %copy-start.19 = (f32[1,121,121]{2,0,1:T(1,128)S(1)}, f32[1,121,121]{2,0,1:T(1,128)}, u32[]{:S(2)}) copy-start(f32[1,121,121]{2,0,1:T(1,128)} %get-tuple-element.20) | copy-start | bytes 175696
  65.8 15.0 %copy-start.58 = (f32[121]{0:T(128)S(1)}, f32[121]{0:T(128)}, u32[]{:S(2)}) copy-start(f32[121]{0:T(128)} %convolution_bitcast_fusion.34) | copy-start | bytes 1456
  65.8 15.8 %copy-start.18 = (f32[1,121,121]{2,0,1:T(1,128)S(1)}, f32[1,121,121]{2,0,1:T(1,128)}, u32[]{:S(2)}) copy-start(f32[1,121,121]{2,0,1:T(1,128)} %get-tuple-element.41) | copy-start | bytes 175696
  65.8 16.1 %copy-start.17 = (f32[1,121,121]{2,0,1:T(1,128)S(1)}, f32[1,121,121]{2,0,1:T(1,128)}, u32[]{:S(2)}) copy-start(f32[1,121,121]{2,0,1:T(1,128)} %get-tuple-element.19) | copy-start | bytes 175696
  65.8 16.1 %copy-start.57 = (f32[121,1]{0,1:T(1,128)S(1)}, f32[121,1]{0,1:T(1,128)}, u32[]{:S(2)}) copy-start(f32[121,1]{0,1:T(1,128)} %copy-done.56) | copy-start | bytes 1456
  65.8 16.3 %copy-start.16 = (f32[1,121,121]{2,0,1:T(1,128)S(1)}, f32[1,121,121]{2,0,1:T(1,128)}, u32[]{:S(2)}) copy-start(f32[1,121,121]{2,0,1:T(1,128)} %get-tuple-element.40) | copy-start | bytes 175696
  65.8 16.5 %copy-start.15 = (f32[1,121,121]{2,0,1:T(1,128)S(1)}, f32[1,121,121]{2,0,1:T(1,128)}, u32[]{:S(2)}) copy-start(f32[1,121,121]{2,0,1:T(1,128)} %get-tuple-element.18) | copy-start | bytes 175696
  65.9 16.5 %copy-start.55 = (f32[121,1]{0,1:T(1,128)S(1)}, f32[121,1]{0,1:T(1,128)}, u32[]{:S(2)}) copy-start(f32[121,1]{0,1:T(1,128)} %copy-done.54) | copy-start | bytes 1456
  65.9 16.7 %copy-start.14 = (f32[1,121,121]{2,0,1:T(1,128)S(1)}, f32[1,121,121]{2,0,1:T(1,128)}, u32[]{:S(2)}) copy-start(f32[1,121,121]{2,0,1:T(1,128)} %get-tuple-element.39) | copy-start | bytes 175696
  65.9 16.9 %copy-start.13 = (f32[1,121,121]{2,0,1:T(1,128)S(1)}, f32[1,121,121]{2,0,1:T(1,128)}, u32[]{:S(2)}) copy-start(f32[1,121,121]{2,0,1:T(1,128)} %get-tuple-element.17) | copy-start | bytes 175696
  65.9 16.9 %copy-start.53 = (f32[121,1]{0,1:T(1,128)S(1)}, f32[121,1]{0,1:T(1,128)}, u32[]{:S(2)}) copy-start(f32[121,1]{0,1:T(1,128)} %copy-done.52) | copy-start | bytes 1456
  65.9 17.1 %copy-start.12 = (f32[1,121,121]{2,0,1:T(1,128)S(1)}, f32[1,121,121]{2,0,1:T(1,128)}, u32[]{:S(2)}) copy-start(f32[1,121,121]{2,0,1:T(1,128)} %get-tuple-element.38) | copy-start | bytes 175696
  65.9 17.3 %copy-start.11 = (f32[1,121,121]{2,0,1:T(1,128)S(1)}, f32[1,121,121]{2,0,1:T(1,128)}, u32[]{:S(2)}) copy-start(f32[1,121,121]{2,0,1:T(1,128)} %get-tuple-element.16) | copy-start | bytes 175696
  65.9 17.3 %copy-start.51 = (f32[121,1]{0,1:T(1,128)S(1)}, f32[121,1]{0,1:T(1,128)}, u32[]{:S(2)}) copy-start(f32[121,1]{0,1:T(1,128)} %copy-done.50) | copy-start | bytes 1456
  65.9 17.6 %copy-start.10 = (f32[1,121,121]{2,0,1:T(1,128)S(1)}, f32[1,121,121]{2,0,1:T(1,128)}, u32[]{:S(2)}) copy-start(f32[1,121,121]{2,0,1:T(1,128)} %get-tuple-element.37) | copy-start | bytes 175696
  65.9 17.8 %copy-start.9 = (f32[1,121,121]{2,0,1:T(1,128)S(1)}, f32[1,121,121]{2,0,1:T(1,128)}, u32[]{:S(2)}) copy-start(f32[1,121,121]{2,0,1:T(1,128)} %get-tuple-element.15) | copy-start | bytes 175696
  65.9 17.8 %copy-start.49 = (f32[121,1]{0,1:T(1,128)S(1)}, f32[121,1]{0,1:T(1,128)}, u32[]{:S(2)}) copy-start(f32[121,1]{0,1:T(1,128)} %copy-done.48) | copy-start | bytes 1456
  66.0 18.0 %copy-start.8 = (f32[1,121,121]{2,0,1:T(1,128)S(1)}, f32[1,121,121]{2,0,1:T(1,128)}, u32[]{:S(2)}) copy-start(f32[1,121,121]{2,0,1:T(1,128)} %get-tuple-element.36) | copy-start | bytes 175696
  66.0 18.2 %copy-start.7 = (f32[1,121,121]{2,0,1:T(1,128)S(1)}, f32[1,121,121]{2,0,1:T(1,128)}, u32[]{:S(2)}) copy-start(f32[1,121,121]{2,0,1:T(1,128)} %get-tuple-element.14) | copy-start | bytes 175696
  66.0 18.2 %copy-start.47 = (f32[121,1]{0,1:T(1,128)S(1)}, f32[121,1]{0,1:T(1,128)}, u32[]{:S(2)}) copy-start(f32[121,1]{0,1:T(1,128)} %copy-done.46) | copy-start | bytes 1456
  66.0 18.9 %copy-start.35 = (f32[121,2]{0,1:T(2,128)S(1)}, f32[121,2]{0,1:T(2,128)}, u32[]{:S(2)}) copy-start(f32[121,2]{0,1:T(2,128)} %copy-done.34) | copy-start | bytes 2908
  66.0 19.8 %copy-start.45 = (f32[121,2]{0,1:T(2,128)S(1)}, f32[121,2]{0,1:T(2,128)}, u32[]{:S(2)}) copy-start(f32[121,2]{0,1:T(2,128)} %copy-done.44) | copy-start | bytes 2908
  66.0 20.0 %copy-start.43 = (f32[121,2]{0,1:T(2,128)S(1)}, f32[121,2]{0,1:T(2,128)}, u32[]{:S(2)}) copy-start(f32[121,2]{0,1:T(2,128)} %copy-done.42) | copy-start | bytes 2908
  66.0 20.7 %copy-start.39 = (f32[121,4]{0,1:T(4,128)S(1)}, f32[121,4]{0,1:T(4,128)}, u32[]{:S(2)}) copy-start(f32[121,4]{0,1:T(4,128)} %copy-done.38) | copy-start | bytes 5812
  66.0 20.9 %copy-start.37 = (f32[121,4]{0,1:T(4,128)S(1)}, f32[121,4]{0,1:T(4,128)}, u32[]{:S(2)}) copy-start(f32[121,4]{0,1:T(4,128)} %copy-done.36) | copy-start | bytes 5812
  80.7 6.9 %copy-start.31 = (f32[121,8]{0,1:T(8,128)S(1)}, f32[121,8]{0,1:T(8,128)}, u32[]{:S(2)}) copy-start(f32[121,8]{0,1:T(8,128)} %copy-done.30) | copy-start | bytes 11620
  80.7 7.1 %copy-start.29 = (f32[121,8]{0,1:T(8,128)S(1)}, f32[121,8]{0,1:T(8,128)}, u32[]{:S(2)}) copy-start(f32[121,8]{0,1:T(8,128)} %copy-done.28) | copy-start | bytes 11620
  80.7 7.8 %copy-start.27 = (f32[121,16]{0,1:T(8,128)S(1)}, f32[121,16]{0,1:T(8,128)}, u32[]{:S(2)}) copy-start(f32[121,16]{0,1:T(8,128)} %copy-done.26) | copy-start | bytes 23236
  80.7 9.0 %copy-start.25 = (f32[121,32]{0,1:T(8,128)S(1)}, f32[121,32]{0,1:T(8,128)}, u32[]{:S(2)}) copy-start(f32[121,32]{0,1:T(8,128)} %copy-done.24) | copy-start | bytes 46468
  80.8 10.0 %copy-start.6 = (f32[121,64]{0,1:T(8,128)S(1)}, f32[121,64]{0,1:T(8,128)}, u32[]{:S(2)}) copy-start(f32[121,64]{0,1:T(8,128)} %copy-done.5) | copy-start | bytes 92932
  85.7 6.0 %copy-start.1 = (bf16[6912,128]{1,0:T(8,128)(2,1)S(1)}, bf16[6912,128]{1,0:T(8,128)(2,1)}, u32[]{:S(2)}) copy-start(bf16[6912,128]{1,0:T(8,128)(2,1)} %gather_fusion) | copy-start | bytes 5308420
  85.8 6.0 %copy-start.4 = (f32[256,128]{1,0:T(8,128)S(1)}, f32[256,128]{1,0:T(8,128)}, u32[]{:S(2)}) copy-start(f32[256,128]{1,0:T(8,128)} %convolution_bitcast_fusion) | copy-start | bytes 393220
  85.8 6.0 %copy-start.32 = (bf16[128,121]{1,0:T(8,128)(2,1)S(1)}, bf16[128,121]{1,0:T(8,128)(2,1)}, u32[]{:S(2)}) copy-start(bf16[128,121]{1,0:T(8,128)(2,1)} %param.17) | copy-start | bytes 92932
  (2 other events, 1.2 us)

commit v2 on v1

v2 whole, which is shorter than its diff:
```python
import jax
import jax.numpy as jnp
from jax import lax
from jax.experimental import pallas as pl
from jax.experimental.pallas import tpu as pltpu
from jax.sharding import PartitionSpec as P

N = 128
CELLS = 256
COEF = 121
ELEM = 128
FAR = 32
SLOTS = 128
HALO = 32
KINDS = 27
NEAR = 9
CLOSE = (1, 2, 3, 4, 124, 125, 126, 127)
FIRST = 5
COUNT = 119
ORDER = tuple(FIRST + i * 37 % COUNT for i in range(COUNT))
GROUP = 8
OWN_AT, CLOSE_AT, FAR_AT = 0, CELLS, CELLS + 8 * SLOTS
ROWS = FAR_AT + N * FAR
LEVEL_AT = (None, 0, 128, 192, 224, 240, 248, 252, 254)
BLOCK_AT = (0, 128, 192, 224, 240, 248, 252)
f32 = jnp.float32
bf16 = jnp.bfloat16
i32 = jnp.int32
MESH = pl.DeviceIdType.MESH
NT = (((1,), (1,)), ((), ()))
TN = (((0,), (0,)), ((), ()))


def mm(a, b):
    return jnp.dot(a, b, preferred_element_type=f32)


def split(x):
    high = x.astype(bf16)
    return high, (x - high.astype(f32)).astype(bf16)


def tripled(x):
    high, low = split(x)
    return jnp.concatenate([high, high, low], axis=1)


def onehot(index, count, axis, shape):
    return (index == lax.broadcasted_iota(i32, shape, axis)).astype(f32).astype(bf16)


def step_kernel(slip_hbm, wm_hbm, up_hbm, down_hbm, sib_hbm, leaf_hbm, ts_hbm, blocks_hbm, send_hbm, far_hbm, near_hbm,
                out_ref,
                slip, wm, up, down, sib, leaf, ts, blocks, send, far_list, near_list,
                wp, tsp, pad, up3, down3, sib3, leafp,
                sendbuf, closebuf, closein, halobuf, haloin, farin, rootbuf, roots,
                agg, blockagg, sibterm0, sibterm1, local, near_acc, indices, table, smem,
                load_sem, send_sem, far_sem, close_sem, halo_sem, root_sem, smem_sem):
    me = lax.axis_index("leaf")
    pairs = ((slip_hbm, slip), (wm_hbm, wm), (send_hbm, send), (up_hbm, up), (down_hbm, down), (sib_hbm, sib),
             (far_hbm, far_list), (near_hbm, near_list), (blocks_hbm, blocks), (ts_hbm, ts), (leaf_hbm, leaf))
    loads = [pltpu.make_async_copy(a, b, load_sem.at[i]) for i, (a, b) in enumerate(pairs)]
    for load in loads:
        load.start()
    barrier = pltpu.get_barrier_semaphore()

    def hello(k, carry):
        pl.semaphore_signal(barrier, inc=1, device_id=(lax.rem(me + k, N),), device_id_type=MESH)
        return carry

    lax.fori_loop(1, N, hello, 0)

    wp[...] = jnp.zeros_like(wp)
    loads[0].wait()
    loads[1].wait()
    wp[0:COEF, :] = wm[...]
    mt = lax.dot_general(slip[...], wp[...], (((0,), (1,)), ((), ())), preferred_element_type=f32).astype(bf16)
    for side in range(2):
        pick = onehot(lax.broadcasted_iota(i32, (HALO, CELLS), 0) + (CELLS - HALO) * (1 - side), CELLS, 1, (HALO, CELLS))
        halobuf[side] = lax.dot_general(pick, slip[...], NT, preferred_element_type=f32).astype(bf16)

    loads[2].wait()
    lists = pltpu.roll(send[...].astype(f32).T, lax.rem(N - me, N), 1)
    lane = lax.broadcasted_iota(i32, (SLOTS, CELLS), 1).astype(f32)

    def peer(k):
        return (lax.rem(me + k, N),)

    def far_copy(k):
        return pltpu.make_async_remote_copy(
            src_ref=sendbuf.at[k], dst_ref=farin.at[me], send_sem=send_sem.at[0], recv_sem=far_sem,
            device_id=peer(k), device_id_type=MESH)

    def close_copy(i):
        return pltpu.make_async_remote_copy(
            src_ref=closebuf.at[i], dst_ref=closein.at[i], send_sem=send_sem.at[1], recv_sem=close_sem,
            device_id=peer(CLOSE[i]), device_id_type=MESH)

    def halo_copy(side):
        return pltpu.make_async_remote_copy(
            src_ref=halobuf.at[side], dst_ref=haloin.at[side], send_sem=send_sem.at[2], recv_sem=halo_sem,
            device_id=peer((1, N - 1)[side]), device_id_type=MESH)

    def root_copy(k):
        return pltpu.make_async_remote_copy(
            src_ref=rootbuf, dst_ref=roots.at[me], send_sem=send_sem.at[3], recv_sem=root_sem,
            device_id=peer(k), device_id_type=MESH)

    def fill(ks):
        for k in ks:
            hot = (lists[0:FAR, k:k + 1] == lane[0:FAR]).astype(f32).astype(bf16)
            sendbuf[k] = mm(hot, mt).astype(bf16)

    groups = [ORDER[i:i + GROUP] for i in range(0, COUNT, GROUP)]
    for i, k in enumerate(CLOSE):
        hot = (lists[:, k:k + 1] == lane).astype(f32).astype(bf16)
        closebuf[i] = mm(hot, mt).astype(bf16)
    fill(groups[0])
    pl.semaphore_wait(barrier, N - 1)
    for side in range(2):
        halo_copy(side).start()
    for i in range(8):
        close_copy(i).start()
    half = len(groups) // 2
    for g in range(half):
        fill(groups[g + 1])
        for k in groups[g]:
            far_copy(k).start()

    pad[...] = jnp.zeros_like(pad)

    def padded_t(ref, s):
        pad[0:COEF, 0:COEF] = ref[:, s, :]
        return split(pad[...].T)

    loads[3].wait()
    for s in range(2):
        high, low = padded_t(up, s)
        up3[s * 128:s * 128 + 128, :] = high
        up3[256 + s * 128:256 + s * 128 + 128, :] = low
        up3[512 + s * 128:512 + s * 128 + 128, :] = high

    def pair_up(ref, at, count):
        pair = jnp.concatenate([ref[pl.ds(at, count, stride=2), :], ref[pl.ds(at + 1, count, stride=2), :]], axis=1)
        return mm(tripled(pair), up3[...])

    table[OWN_AT:OWN_AT + CELLS, :] = mt.astype(f32)
    agg[248:256, :] = jnp.zeros((8, 128), f32)
    agg[0:128, :] = pair_up(table, OWN_AT, 128)
    for level in range(1, 8):
        count = 128 >> level
        agg[pl.ds(LEVEL_AT[level + 1], count), :] = pair_up(agg, LEVEL_AT[level], count)
    root = agg[pl.ds(LEVEL_AT[8], 1), :]
    rootbuf[...] = root
    roots[me] = root

    for g in range(half, len(groups)):
        if g + 1 < len(groups):
            fill(groups[g + 1])
        for k in groups[g]:
            far_copy(k).start()
        if g == half:
            def tell(k, carry):
                root_copy(k).start()
                return carry
            lax.fori_loop(1, N, tell, 0)

    for load, ref, ref3 in ((loads[4], down, down3), (loads[5], sib, sib3)):
        load.wait()
        for s in range(2):
            high, low = padded_t(ref, s)
            ref3[0:128, s * 128:s * 128 + 128] = high
            ref3[128:256, s * 128:s * 128 + 128] = low
            ref3[256:384, s * 128:s * 128 + 128] = high
    sibs = mm(tripled(agg[...]), sib3[...])
    sibterm0[...] = sibs[:, 0:128]
    sibterm1[...] = sibs[:, 128:256]

    loads[6].wait()
    entry = far_list[...]
    rel = entry - CELLS
    sender = rel // SLOTS
    slot = rel - sender * SLOTS
    off = (me - sender) & (N - 1)
    close = jnp.where(off <= 4, off - 1, off - 120)
    is_close = (off <= 4) | (off >= 124)
    row = jnp.where(is_close, CLOSE_AT + close * SLOTS + slot, FAR_AT + sender * FAR + slot)
    indices[...] = jnp.where(entry < CELLS, entry, row)
    to_smem = pltpu.make_async_copy(indices, smem, smem_sem)
    to_smem.start()

    loads[7].wait()
    loads[8].wait()
    loads[9].wait()
    pltpu.make_async_copy(halobuf, haloin, halo_sem).wait()
    left = jnp.where(me > 0, haloin[0].astype(f32), 0.0)
    right = jnp.where(me < N - 1, haloin[1].astype(f32), 0.0)
    edge = jnp.concatenate([left, right], axis=0).T.astype(bf16)
    own = slip[...]
    near_acc[...] = jnp.zeros_like(near_acc)
    for k in range(NEAR):
        w = near_list[k:k + 1, :]
        at = jnp.where(w < HALO, w + CELLS, jnp.where(w < HALO + CELLS, w - HALO, w))
        hot = onehot(at, 0, 0, (CELLS + 2 * HALO, CELLS))
        cols = mm(own, hot[0:CELLS]) + mm(edge, hot[CELLS:])
        near_acc[...] += mm(blocks[k], cols.astype(bf16))
    tsp[...] = jnp.zeros_like(tsp)
    tsp[:, 0:COEF] = ts[...]

    pltpu.make_async_copy(roots.at[0:N - 1], roots.at[0:N - 1], root_sem).wait()
    blockagg[0:N, :] = roots[...].reshape(N, 128)
    for bit in range(6):
        count = 64 >> bit
        blockagg[pl.ds(BLOCK_AT[bit + 1], count), :] = pair_up(blockagg, BLOCK_AT[bit], count)
    branch = [(me >> bit) & 1 for bit in range(7)]
    rows = [blockagg[pl.ds(BLOCK_AT[bit] + ((me >> bit) ^ 1), 1), :] for bit in range(7)]
    terms = mm(tripled(jnp.concatenate(rows + [rows[0]], axis=0)), sib3[...])
    expansion = jnp.zeros((8, 128), f32)
    for bit in reversed(range(7)):
        both = jnp.broadcast_to(terms[bit:bit + 1, :], (8, 256))
        if bit < 6:
            both = both + mm(tripled(expansion), down3[...])
        expansion = jnp.where(branch[bit] == 0, both[:, 0:128], both[:, 128:256])

    local[0:8, :] = jnp.zeros((8, 128), f32)
    for level in reversed(range(8)):
        count = 128 >> level
        both = mm(tripled(expansion), down3[...])
        low, high = both[0:count, 0:128], both[0:count, 128:256]
        if level >= 1:
            at = LEVEL_AT[level]
            low = low + sibterm0[pl.ds(at + 1, count, stride=2), :]
            high = high + sibterm1[pl.ds(at, count, stride=2), :]
        local[pl.ds(0, count, stride=2), :] = low
        local[pl.ds(1, count, stride=2), :] = high
        expansion = local[0:max(2 * count, 8), :]

    leafp[...] = jnp.zeros_like(leafp)
    loads[10].wait()
    for t in range(KINDS):
        leafp[t, 0:COEF, 0:COEF] = leaf[t]

    pltpu.make_async_copy(closebuf, closein, close_sem).wait()
    for i in range(8):
        table[CLOSE_AT + i * SLOTS:CLOSE_AT + (i + 1) * SLOTS, :] = closein[i].astype(f32)
    to_smem.wait()
    pltpu.make_async_copy(farin.at[0:COUNT], farin.at[0:COUNT], far_sem).wait()

    def widen(q, carry):
        for j in range(4):
            table[pl.ds(pl.multiple_of(FAR_AT + (q * 4 + j) * FAR, FAR), FAR), :] = farin[q * 4 + j].astype(f32)
        return carry

    lax.fori_loop(0, N // 4, widen, 0)

    sub = lax.broadcasted_iota(i32, (8, 128), 0)
    total = local[...]
    for t in range(KINDS):
        parts = []
        for b in range(CELLS // 8):
            v = jnp.broadcast_to(table[pl.ds(smem[t, b * 8], 1), :], (8, 128))
            for j in range(1, 8):
                r = jnp.broadcast_to(table[pl.ds(smem[t, b * 8 + j], 1), :], (8, 128))
                v = jnp.where(sub == j, r, v)
            parts.append(v)
        rows = jnp.concatenate(parts, axis=0).astype(bf16)
        total = total + lax.dot_general(rows, leafp[t], NT, preferred_element_type=f32)
    stress = lax.dot_general(tsp[...], total.astype(bf16), NT, preferred_element_type=f32)
    out_ref[...] = stress + near_acc[...]

    pltpu.make_async_copy(halobuf, halobuf, send_sem.at[2]).wait()
    pltpu.make_async_copy(closebuf, closebuf, send_sem.at[1]).wait()
    pltpu.make_async_copy(roots.at[0:N - 1], roots.at[0:N - 1], send_sem.at[3]).wait()
    pltpu.make_async_copy(sendbuf.at[0:COUNT], sendbuf.at[0:COUNT], send_sem.at[0]).wait()


def body(slip, to_multipole, up_shift, down_shift, sibling_far, leaf_far, to_stress, near_blocks,
         send_cells, far_list, near_list):
    up_shift, down_shift, sibling_far = (x.transpose(1, 0, 2) for x in (up_shift, down_shift, sibling_far))
    args = (slip, to_multipole, up_shift, down_shift, sibling_far, leaf_far, to_stress, near_blocks,
            send_cells.reshape(N, SLOTS), far_list, near_list)
    anywhere = pl.BlockSpec(memory_space=pl.ANY)
    return pl.pallas_call(
        step_kernel,
        out_shape=jax.ShapeDtypeStruct((ELEM, CELLS), f32),
        in_specs=[anywhere] * len(args),
        out_specs=pl.BlockSpec(memory_space=pltpu.VMEM),
        scratch_shapes=[pltpu.VMEM(a.shape, a.dtype) for a in args] + [
            pltpu.VMEM((128, 128), bf16),
            pltpu.VMEM((128, 128), bf16),
            pltpu.VMEM((128, 128), f32),
            pltpu.VMEM((768, 128), bf16),
            pltpu.VMEM((384, 256), bf16),
            pltpu.VMEM((384, 256), bf16),
            pltpu.VMEM((KINDS, 128, 128), bf16),
            pltpu.VMEM((N, FAR, 128), bf16),
            pltpu.VMEM((8, SLOTS, 128), bf16),
            pltpu.VMEM((8, SLOTS, 128), bf16),
            pltpu.VMEM((2, HALO, ELEM), bf16),
            pltpu.VMEM((2, HALO, ELEM), bf16),
            pltpu.VMEM((N, FAR, 128), bf16),
            pltpu.VMEM((1, 128), f32),
            pltpu.VMEM((N, 1, 128), f32),
            pltpu.VMEM((256, 128), f32),
            pltpu.VMEM((256, 128), f32),
            pltpu.VMEM((256, 128), f32),
            pltpu.VMEM((256, 128), f32),
            pltpu.VMEM((256, 128), f32),
            pltpu.VMEM((ELEM, CELLS), f32),
            pltpu.VMEM((KINDS, CELLS), i32),
            pltpu.VMEM((ROWS, 128), f32),
            pltpu.SMEM((KINDS, CELLS), i32),
            pltpu.SemaphoreType.DMA((len(args),)),
            pltpu.SemaphoreType.DMA((4,)),
            pltpu.SemaphoreType.DMA,
            pltpu.SemaphoreType.DMA,
            pltpu.SemaphoreType.DMA,
            pltpu.SemaphoreType.DMA,
            pltpu.SemaphoreType.DMA,
        ],
        compiler_params=pltpu.CompilerParams(collective_id=0, has_side_effects=True),
        name="step",
    )(*args)


def solution(mesh):
    cut = P(None, "leaf")
    return jax.shard_map(body, mesh=mesh,
                         in_specs=(cut, P(), P(), P(), P(), P(), P(), P(), P("leaf", None), cut, cut),
                         out_specs=cut, check_vma=False)
```

time: 93.6 us -> 38.2 us (0.41)
  the two profiles are of different devices: /device:TPU:0 before, /device:TPU:1 now
where the time goes in v2:
time: 38.2 us; the launch traced here: 38.1 us
  Pallas kernels  36.5 us (96%)
  local copies, waits for them, and re-layouts  1.57 us (4%)
    pallas_call x1, Pallas kernels, body(): pl.pallas_call(step_kernel, out_shape=jax.ShapeDtypeStruct((ELEM, CELLS),...  36.5 us
    unnamed x1, local copies, waits for them, and re-layouts  1.57 us

profile of v2, /device:TPU:1, one launch (start us, length us, event | category | flops | bytes accessed | tf_op | source)
XLA Modules:
  0.0 38.1 jit_solution(8438979356918490373)
XLA Ops:
  0.0 36.5 %step.1 = f32[128,256]{1,0:T(8,128)} custom-call(bf16[128,256]{1,0:T(8,128)(2,1)} %slip_hbm.1, bf16[121,128]{1,0:T(8,128)(2,1)} %wm_hbm.1, f32[121,2,121]{2,1,0:T(2,128)} %bitcast.4, f32[121,2,121]{2,1,0:T(2,128)} %bitcast.5, f32[121,2,121]{2,1,0:T(2,128)} %bitcast.6, bf16[27,121,121]{2,1,0:T(8,128)(2,1)} %leaf_hbm.1, bf16[128,121]{1,0:T(8,128)(2,1)} %ts_hbm.1, ...), custom_call_target="tpu_custom_call" | custom-call | tf_op jit(solution)/shard_map/step/pallas_call | solution.py:283
  36.5 1.6 %copy.13 = f32[128,256]{1,0:T(8,128)} copy(f32[128,256]{1,0:T(8,128)} %step.1) | data formatting | bytes 262144

commit v3 on v2

--- a/solution.py
+++ b/solution.py
@@ -17,8 +17,17 @@
 CLOSE = (1, 2, 3, 4, 124, 125, 126, 127)
 FIRST = 5
 COUNT = 119
-ORDER = tuple(FIRST + i * 37 % COUNT for i in range(COUNT))
-GROUP = 8
+
+
+def hops(k):
+    return sum(min(k // d % 4, 4 - k // d % 4) for d in (32, 8, 2))
+
+
+ORDER = tuple(sorted((FIRST + i * 37 % COUNT for i in range(COUNT)), key=lambda k: -hops(k)))
+ROOTS_AFTER = 12
+CUTS = (0, 30, 60, 90, 105, COUNT)
+CLASS = {k: j for j in range(len(CUTS) - 1) for k in ORDER[CUTS[j]:CUTS[j + 1]]}
+CLOSE_AFTER = 60
 OWN_AT, CLOSE_AT, FAR_AT = 0, CELLS, CELLS + 8 * SLOTS
 ROWS = FAR_AT + N * FAR
 LEVEL_AT = (None, 0, 128, 192, 224, 240, 248, 252, 254)
@@ -88,7 +97,7 @@
 
     def far_copy(k):
         return pltpu.make_async_remote_copy(
-            src_ref=sendbuf.at[k], dst_ref=farin.at[me], send_sem=send_sem.at[0], recv_sem=far_sem,
+            src_ref=sendbuf.at[k], dst_ref=farin.at[k], send_sem=send_sem.at[0], recv_sem=far_sem.at[CLASS[k]],
             device_id=peer(k), device_id_type=MESH)
 
     def close_copy(i):
@@ -111,21 +120,10 @@
             hot = (lists[0:FAR, k:k + 1] == lane[0:FAR]).astype(f32).astype(bf16)
             sendbuf[k] = mm(hot, mt).astype(bf16)
 
-    groups = [ORDER[i:i + GROUP] for i in range(0, COUNT, GROUP)]
     for i, k in enumerate(CLOSE):
         hot = (lists[:, k:k + 1] == lane).astype(f32).astype(bf16)
         closebuf[i] = mm(hot, mt).astype(bf16)
-    fill(groups[0])
-    pl.semaphore_wait(barrier, N - 1)
-    for side in range(2):
-        halo_copy(side).start()
-    for i in range(8):
-        close_copy(i).start()
-    half = len(groups) // 2
-    for g in range(half):
-        fill(groups[g + 1])
-        for k in groups[g]:
-            far_copy(k).start()
+    fill(ORDER)
 
     pad[...] = jnp.zeros_like(pad)
 
@@ -154,16 +152,22 @@
     rootbuf[...] = root
     roots[me] = root
 
-    for g in range(half, len(groups)):
-        if g + 1 < len(groups):
-            fill(groups[g + 1])
-        for k in groups[g]:
-            far_copy(k).start()
-        if g == half:
-            def tell(k, carry):
-                root_copy(k).start()
-                return carry
+    pl.semaphore_wait(barrier, N - 1)
+
+    def tell(k, carry):
+        root_copy(k).start()
+        return carry
+
+    for i in range(COUNT + 1):
+        if i == 10:
+            for side in range(2):
+                halo_copy(side).start()
+        if i % 12 == 11 and i // 12 < 8:
+            close_copy(i // 12).start()
+        if i == ROOTS_AFTER:
             lax.fori_loop(1, N, tell, 0)
+        if i < COUNT:
+            far_copy(ORDER[i]).start()
 
     for load, ref, ref3 in ((loads[4], down, down3), (loads[5], sib, sib3)):
         load.wait()
@@ -184,7 +188,7 @@
     off = (me - sender) & (N - 1)
     close = jnp.where(off <= 4, off - 1, off - 120)
     is_close = (off <= 4) | (off >= 124)
-    row = jnp.where(is_close, CLOSE_AT + close * SLOTS + slot, FAR_AT + sender * FAR + slot)
+    row = jnp.where(is_close, CLOSE_AT + close * SLOTS + slot, FAR_AT + off * FAR + slot)
     indices[...] = jnp.where(entry < CELLS, entry, row)
     to_smem = pltpu.make_async_copy(indices, smem, smem_sem)
     to_smem.start()
@@ -244,14 +248,11 @@
     for i in range(8):
         table[CLOSE_AT + i * SLOTS:CLOSE_AT + (i + 1) * SLOTS, :] = closein[i].astype(f32)
     to_smem.wait()
-    pltpu.make_async_copy(farin.at[0:COUNT], farin.at[0:COUNT], far_sem).wait()
-
-    def widen(q, carry):
-        for j in range(4):
-            table[pl.ds(pl.multiple_of(FAR_AT + (q * 4 + j) * FAR, FAR), FAR), :] = farin[q * 4 + j].astype(f32)
-        return carry
-
-    lax.fori_loop(0, N // 4, widen, 0)
+    for j in range(len(CUTS) - 1):
+        count = CUTS[j + 1] - CUTS[j]
+        pltpu.make_async_copy(farin.at[0:count], farin.at[0:count], far_sem.at[j]).wait()
+        for k in ORDER[CUTS[j]:CUTS[j + 1]]:
+            table[FAR_AT + k * FAR:FAR_AT + (k + 1) * FAR, :] = farin[k].astype(f32)
 
     sub = lax.broadcasted_iota(i32, (8, 128), 0)
     total = local[...]
@@ -282,7 +283,7 @@
     anywhere = pl.BlockSpec(memory_space=pl.ANY)
     return pl.pallas_call(
         step_kernel,
-        out_shape=jax.ShapeDtypeStruct((ELEM, CELLS), f32),
+        out_shape=pltpu.VMEM((ELEM, CELLS), f32),
         in_specs=[anywhere] * len(args),
         out_specs=pl.BlockSpec(memory_space=pltpu.VMEM),
         scratch_shapes=[pltpu.VMEM(a.shape, a.dtype) for a in args] + [
@@ -312,7 +313,7 @@
             pltpu.SMEM((KINDS, CELLS), i32),
             pltpu.SemaphoreType.DMA((len(args),)),
             pltpu.SemaphoreType.DMA((4,)),
-            pltpu.SemaphoreType.DMA,
+            pltpu.SemaphoreType.DMA((len(CUTS) - 1,)),
             pltpu.SemaphoreType.DMA,
             pltpu.SemaphoreType.DMA,
             pltpu.SemaphoreType.DMA,

time: 38.2 us -> 33.7 us (0.88)
  Pallas kernels: 36.5 us -> 32.9 us
  local copies, waits for them, and re-layouts: 1.57 us -> 0.66 us
    pallas_call x1, Pallas kernels: 36.5 us -> 32.9 us  [body(): pl.pallas_call(step_kernel, out_shape=pltpu.VMEM((ELEM, CELLS), f32), in_...]
    unnamed x1, local copies, waits for them, and re-layouts: 1.57 us -> 0.66 us
where the time goes in v3:
time: 33.7 us; the launch traced here: 33.6 us
  Pallas kernels  32.9 us (98%)
  local copies, waits for them, and re-layouts  0.66 us (2%)
    pallas_call x1, Pallas kernels, body(): pl.pallas_call(step_kernel, out_shape=pltpu.VMEM((ELEM, CELLS), f32), in_...  32.9 us

profile of v3, /device:TPU:1, one launch (start us, length us, event | category | flops | bytes accessed | tf_op | source)
XLA Modules:
  0.0 33.6 jit_solution(796009000290288043)
XLA Ops:
  0.0 32.9 %step.1 = f32[128,256]{1,0:T(8,128)S(1)} custom-call(bf16[128,256]{1,0:T(8,128)(2,1)} %slip_hbm.1, bf16[121,128]{1,0:T(8,128)(2,1)} %wm_hbm.1, f32[121,2,121]{2,1,0:T(2,128)} %bitcast.4, f32[121,2,121]{2,1,0:T(2,128)} %bitcast.5, f32[121,2,121]{2,1,0:T(2,128)} %bitcast.6, bf16[27,121,121]{2,1,0:T(8,128)(2,1)} %leaf_hbm.1, bf16[128,121]{1,0:T(8,128)(2,1)} %ts_hbm.1, ...), custom_call_target="tpu_custom_call" | custom-call | tf_op jit(solution)/shard_map/step/pallas_call | solution.py:284
  32.9 0.7 %copy.13 = f32[128,256]{1,0:T(8,128)} copy(f32[128,256]{1,0:T(8,128)S(1)} %step.1) | data formatting | bytes 262144

commit v4 on v3

--- a/solution.py
+++ b/solution.py
@@ -24,6 +24,7 @@
 
 
 ORDER = tuple(sorted((FIRST + i * 37 % COUNT for i in range(COUNT)), key=lambda k: -hops(k)))
+ALL = tuple(sorted(range(1, N), key=lambda k: -hops(k)))
 ROOTS_AFTER = 12
 CUTS = (0, 30, 60, 90, 105, COUNT)
 CLASS = {k: j for j in range(len(CUTS) - 1) for k in ORDER[CUTS[j]:CUTS[j + 1]]}
@@ -73,11 +74,8 @@
         load.start()
     barrier = pltpu.get_barrier_semaphore()
 
-    def hello(k, carry):
-        pl.semaphore_signal(barrier, inc=1, device_id=(lax.rem(me + k, N),), device_id_type=MESH)
-        return carry
-
-    lax.fori_loop(1, N, hello, 0)
+    for k in ALL:
+        pl.semaphore_signal(barrier, inc=1, device_id=((me + k) & (N - 1),), device_id_type=MESH)
 
     wp[...] = jnp.zeros_like(wp)
     loads[0].wait()
@@ -89,11 +87,11 @@
         halobuf[side] = lax.dot_general(pick, slip[...], NT, preferred_element_type=f32).astype(bf16)
 
     loads[2].wait()
-    lists = pltpu.roll(send[...].astype(f32).T, lax.rem(N - me, N), 1)
+    lists = pltpu.roll(send[...].astype(f32).T, (N - me) & (N - 1), 1)
     lane = lax.broadcasted_iota(i32, (SLOTS, CELLS), 1).astype(f32)
 
     def peer(k):
-        return (lax.rem(me + k, N),)
+        return ((me + k) & (N - 1),)
 
     def far_copy(k):
         return pltpu.make_async_remote_copy(
@@ -154,10 +152,6 @@
 
     pl.semaphore_wait(barrier, N - 1)
 
-    def tell(k, carry):
-        root_copy(k).start()
-        return carry
-
     for i in range(COUNT + 1):
         if i == 10:
             for side in range(2):
@@ -165,7 +159,8 @@
         if i % 12 == 11 and i // 12 < 8:
             close_copy(i // 12).start()
         if i == ROOTS_AFTER:
-            lax.fori_loop(1, N, tell, 0)
+            for k in ALL:
+                root_copy(k).start()
         if i < COUNT:
             far_copy(ORDER[i]).start()
 

time: 33.7 us -> 32.9 us (0.976)
  Pallas kernels: 32.9 us -> 32.2 us
    pallas_call x1, Pallas kernels: 32.9 us -> 32.2 us  [body(): pl.pallas_call(step_kernel, out_shape=pltpu.VMEM((ELEM, CELLS), f32), in_...]
where the time goes in v4:
time: 32.9 us; the launch traced here: 32.8 us
  Pallas kernels  32.2 us (98%)
  local copies, waits for them, and re-layouts  0.66 us (2%)
    pallas_call x1, Pallas kernels, body(): pl.pallas_call(step_kernel, out_shape=pltpu.VMEM((ELEM, CELLS), f32), in_...  32.2 us

profile of v4, /device:TPU:1, one launch (start us, length us, event | category | flops | bytes accessed | tf_op | source)
XLA Modules:
  0.0 32.8 jit_solution(12603353837830551450)
XLA Ops:
  0.0 32.2 %step.1 = f32[128,256]{1,0:T(8,128)S(1)} custom-call(bf16[128,256]{1,0:T(8,128)(2,1)} %slip_hbm.1, bf16[121,128]{1,0:T(8,128)(2,1)} %wm_hbm.1, f32[121,2,121]{2,1,0:T(2,128)} %bitcast.4, f32[121,2,121]{2,1,0:T(2,128)} %bitcast.5, f32[121,2,121]{2,1,0:T(2,128)} %bitcast.6, bf16[27,121,121]{2,1,0:T(8,128)(2,1)} %leaf_hbm.1, bf16[128,121]{1,0:T(8,128)(2,1)} %ts_hbm.1, ...), custom_call_target="tpu_custom_call" | custom-call | tf_op jit(solution)/shard_map/step/pallas_call | solution.py:279
  32.2 0.7 %copy.13 = f32[128,256]{1,0:T(8,128)} copy(f32[128,256]{1,0:T(8,128)S(1)} %step.1) | data formatting | bytes 262144
